TPU v7x, 32 devices: a whole 2x2x4 slice. The times are simulated.
32 devices in a mesh: seq: 2 (over y), dp: 16 (over z, x, core).
Axes of the slice: x: 2, y: 2, z: 4, core: 2. Of those that a mesh axis runs over, the one named last changes fastest.
Arguments:
- inputs: bfloat16 [16, 2, 1024, 768], P('dp', None, 'seq'), may hold values from -6 to 6
- query_weight: bfloat16 [768, 768], P(('seq', 'dp')), may hold values from -0.21875 to 0.21875
- key_weight: bfloat16 [768, 768], P(('seq', 'dp')), may hold values from -0.21875 to 0.21875
- value_weight: bfloat16 [768, 768], P(('seq', 'dp')), may hold values from -0.21875 to 0.21875
- query_bias: bfloat16 [768], P(('seq', 'dp')), may hold values from -3 to 3
- value_bias: bfloat16 [768], P(('seq', 'dp')), may hold values from -3 to 3
- output_weight: bfloat16 [768, 768], P(('seq', 'dp')), may hold values from -2.5 to 2.5
- output_bias: bfloat16 [768], P(('seq', 'dp')), may hold values from -3 to 3
- first_gain: bfloat16 [768], P(('seq', 'dp')), may hold values from 0.099609375 to 1.8984375
- first_shift: bfloat16 [768], P(('seq', 'dp')), may hold values from -3 to 3
- inner_weight: bfloat16 [768, 3072], P(('seq', 'dp')), may hold values from -0.21875 to 0.21875
- inner_bias: bfloat16 [3072], P(('seq', 'dp')), may hold values from -3 to 3
- outer_weight: bfloat16 [3072, 768], P(('seq', 'dp')), may hold values from -0.109375 to 0.109375
- outer_bias: bfloat16 [768], P(('seq', 'dp')), may hold values from -3 to 3
- second_gain: bfloat16 [768], P(('seq', 'dp')), may hold values from 0.099609375 to 1.8984375
- second_shift: bfloat16 [768], P(('seq', 'dp')), may hold values from -3 to 3
- prefix: int32 [16, 2], P('dp'), may hold values from 102 to 512, as said below
- cotangent: bfloat16 [16, 2, 1024, 768], P('dp', None, 'seq'), may hold values from -6 to 6
Outputs:
- outputs: bfloat16 [16, 2, 1024, 768], P('dp', None, 'seq')
- input_grad: float32 [16, 2, 1024, 768], P('dp', None, 'seq')
- grad_query_weight: float32 [768, 768], P(('seq', 'dp'))
- grad_key_weight: float32 [768, 768], P(('seq', 'dp'))
- grad_value_weight: float32 [768, 768], P(('seq', 'dp'))
- grad_query_bias: float32 [768], P(('seq', 'dp'))
- grad_value_bias: float32 [768], P(('seq', 'dp'))
- grad_output_weight: float32 [768, 768], P(('seq', 'dp'))
- grad_output_bias: float32 [768], P(('seq', 'dp'))
- grad_first_gain: float32 [768], P(('seq', 'dp'))
- grad_first_shift: float32 [768], P(('seq', 'dp'))
- grad_inner_weight: float32 [768, 3072], P(('seq', 'dp'))
- grad_inner_bias: float32 [3072], P(('seq', 'dp'))
- grad_outer_weight: float32 [3072, 768], P(('seq', 'dp'))
- grad_outer_bias: float32 [768], P(('seq', 'dp'))
- grad_second_gain: float32 [768], P(('seq', 'dp'))
- grad_second_shift: float32 [768], P(('seq', 'dp'))
Inputs may be any that keep to these rules, and one draw needn't show every extreme that they name: `prefix`: the number of leading tokens of each sequence that attend to one another both ways; some sequence has 512 and some 1024 // 10.
All inputs are finite; a program needn't handle non-finite values.
Results may differ from a plain program's by a relative error of at most 0.017.
Values may be sent and summed in bfloat16 or wider, within the bound.
A program may use at most 384 MiB of HBM per device.

v0:
```python
import functools

import jax
import jax.numpy as jnp
from jax import lax
from jax.experimental import pallas as pl
from jax.experimental.pallas import tpu as pltpu
from jax.sharding import PartitionSpec as P

HEADS = 12
HEAD_DIM = 64
EPS = 1e-05
BOTH = ("seq", "dp")
F32 = jnp.float32
BF16 = jnp.bfloat16
MESH = pl.DeviceIdType.MESH
LINE = 4
SQUARE = 4
CHIPS = LINE * SQUARE


def device_coords(p, z, core):
    return ((p + 1) // 2) % 2, 4 * z + 2 * (p // 2) + core


def device_index(p, z, core):
    y, dp = device_coords(p, z, core)
    return y * CHIPS + dp


def whereabouts():
    y, dp = lax.axis_index("seq"), lax.axis_index("dp")
    z, x, core = dp // 4, (dp // 2) % 2, dp % 2
    return 2 * x + (x + y) % 2, z, core


def heights(z):
    code = jnp.where(z == 0, 1 + 4 * 2 + 16 * 3, jnp.where(z == 1, 0 + 4 * 2 + 16 * 3, jnp.where(z == 2, 1 + 4 * 3, 2 + 4 * 1)))
    return [z, code % 4, (code // 4) % 4, (code // 16) % 4]


def meet(z, always, up, down):
    barrier = pltpu.get_barrier_semaphore()

    def greet(target):
        pl.semaphore_signal(barrier, inc=1, device_id=target, device_id_type=MESH)

    for target in always:
        greet(target)
    pl.when(z < LINE - 1)(lambda: greet(up))
    pl.when(z > 0)(lambda: greet(down))
    ends = jnp.where(z == 0, 1, 0) + jnp.where(z == LINE - 1, 1, 0)
    pl.semaphore_wait(barrier, len(always) + 2 - ends)


def remote(src, dst, send, recv, target):
    return pltpu.make_async_remote_copy(
        src_ref=src, dst_ref=dst, send_sem=send, recv_sem=recv, device_id=target, device_id_type=MESH
    )


def neighbours():
    p, z, core = whereabouts()
    turn = 1 + 2 * core
    ahead, behind, across = (p + turn) % SQUARE, (p + SQUARE - turn) % SQUARE, (p + 2) % SQUARE
    to_ahead, to_behind = device_coords(ahead, z, core), device_coords(behind, z, core)
    partner = device_coords(p, z, 1 - core)
    up = device_coords(p, jnp.minimum(z + 1, LINE - 1), core)
    down = device_coords(p, jnp.maximum(z - 1, 0), core)
    return p, z, core, ahead, behind, across, to_ahead, to_behind, partner, up, down


def gather_kernel(count, *refs):
    s, o = refs[:count], refs[count : 2 * count]
    sems = refs[2 * count :]
    local_sem, pair_send, pair_recv, up_send, down_send, line_recv = sems[:6]
    one_send, one_recv, two_send, two_recv, far_send, far_recv = sems[6:]
    p, z, core, ahead, behind, across, to_ahead, to_behind, partner, up, down = neighbours()

    def place(k, q, t):
        return o[k].at[device_index(q, t, core)]

    def local(k):
        return pltpu.make_async_copy(s[k], place(k, p, z), local_sem.at[k])

    def to_pair(k, q, t, src):
        return remote(src, place(k, q, t), pair_send.at[k, q, t], pair_recv.at[k, q, t], partner)

    def rise(k, t, src):
        return remote(src, place(k, p, t), up_send.at[k, t], line_recv.at[k, t], up)

    def sink(k, t, src):
        return remote(src, place(k, p, t), down_send.at[k, t], line_recv.at[k, t], down)

    def one(k, t, src):
        return remote(src, place(k, p, t), one_send.at[k, t], one_recv.at[k, t], to_ahead)

    def two(k, t, src):
        return remote(src, place(k, p, t), two_send.at[k, t], two_recv.at[k, t], to_behind)

    def far(k, t, src):
        return remote(src, place(k, behind, t), far_send.at[k, t], far_recv.at[k, t], to_ahead)

    meet(z, (to_ahead, to_behind, partner), up, down)
    order = heights(z)

    def spread(k, t, src):
        pl.when((t <= z) & (z < LINE - 1))(lambda: rise(k, t, src).start())
        pl.when((t >= z) & (z > 0))(lambda: sink(k, t, src).start())
        one(k, t, src).start()
        two(k, t, src).start()
        to_pair(k, p, t, src).start()

    def column(k, t):
        rise(k, t, place(k, p, t)).wait_recv()
        spread(k, t, place(k, p, t))

    def sides(k, t):
        one(k, t, place(k, behind, t)).wait_recv()
        far(k, t, place(k, behind, t)).start()
        to_pair(k, behind, t, place(k, behind, t)).start()
        two(k, t, place(k, ahead, t)).wait_recv()
        to_pair(k, ahead, t, place(k, ahead, t)).start()

    def corner(k, t):
        far(k, t, place(k, across, t)).wait_recv()
        to_pair(k, across, t, place(k, across, t)).start()

    for k in range(count):
        spread(k, z, s[k])
        local(k).start()
    for i in range(1, LINE):
        for k in range(count):
            column(k, order[i])
            sides(k, order[i - 1])
            if i > 1:
                corner(k, order[i - 2])
    for k in range(count):
        sides(k, order[LINE - 1])
        corner(k, order[LINE - 2])
    for k in range(count):
        corner(k, order[LINE - 1])

    def drain(i, _):
        q, t = i // LINE, i % LINE
        for k in range(count):
            copy = to_pair(k, q, t, place(k, q, t))
            copy.wait_send()
            copy.wait_recv()
        return 0

    lax.fori_loop(0, CHIPS, drain, 0)

    def drain_line(t, _):
        for k in range(count):
            src = place(k, p, t)
            pl.when((t <= z) & (z < LINE - 1))(lambda: rise(k, t, src).wait_send())
            pl.when((t >= z) & (z > 0))(lambda: sink(k, t, src).wait_send())
            one(k, t, src).wait_send()
            two(k, t, src).wait_send()
            far(k, t, src).wait_send()
        return 0

    lax.fori_loop(0, LINE, drain_line, 0)
    for k in range(count):
        local(k).wait()


def grid_gather(parts, collective_id):
    count = len(parts)
    dma = lambda *n: pltpu.SemaphoreType.DMA((count,) + n)
    return pl.pallas_call(
        functools.partial(gather_kernel, count),
        out_shape=[jax.ShapeDtypeStruct((2 * CHIPS,) + p.shape, p.dtype) for p in parts],
        in_specs=[pl.BlockSpec(memory_space=pltpu.VMEM)] * count,
        out_specs=[pl.BlockSpec(memory_space=pl.ANY)] * count,
        scratch_shapes=[dma(), dma(SQUARE, LINE), dma(SQUARE, LINE)] + [dma(LINE)] * 9,
        compiler_params=pltpu.CompilerParams(collective_id=collective_id, has_side_effects=True),
        name="grid_gather",
    )(*parts)


def scatter_kernel(count, *refs):
    g, out = refs[:count], refs[count : 2 * count]
    own, pair, far_in, one_in, two_in, up_in, down_in = [
        refs[(2 + i) * count : (3 + i) * count] for i in range(7)
    ]
    sems = refs[9 * count :]
    local_sem, pair_send, pair_recv = sems[:3]
    far_send, far_recv, one_send, one_recv, two_send, two_recv, up_send, up_recv, down_send, down_recv = sems[3:]
    p, z, core, ahead, behind, across, to_ahead, to_behind, partner, up, down = neighbours()

    def local(k, q, t):
        return pltpu.make_async_copy(g[k].at[device_index(q, t, core)], own[k].at[q, t], local_sem.at[k, q, t])

    def to_pair(k, q, t):
        return remote(
            g[k].at[device_index(q, t, 1 - core)],
            pair[k].at[q, t],
            pair_send.at[k, q, t],
            pair_recv.at[k, q, t],
            partner,
        )

    def far(k, t, src):
        return remote(src, far_in[k].at[t], far_send.at[k, t], far_recv.at[k, t], to_behind)

    def one(k, t, src):
        return remote(src, one_in[k].at[t], one_send.at[k, t], one_recv.at[k, t], to_behind)

    def two(k, t, src):
        return remote(src, two_in[k].at[t], two_send.at[k, t], two_recv.at[k, t], to_ahead)

    def rise(k, t, src):
        return remote(src, up_in[k].at[t], up_send.at[k, t], up_recv.at[k, t], up)

    def sink(k, t, src):
        return remote(src, down_in[k].at[t], down_send.at[k, t], down_recv.at[k, t], down)

    def term(k, q, t):
        local(k, q, t).wait()
        to_pair(k, q, t).wait_recv()
        return own[k][q, t].astype(F32) + pair[k][q, t].astype(F32)

    meet(z, (to_ahead, to_behind, partner), up, down)
    order = heights(z)[::-1]
    for t in order:
        for q in (across, behind, ahead, p):
            for k in range(count):
                to_pair(k, q, t).start()
                local(k, q, t).start()

    def open_square(k, t):
        pair[k][across, t] = term(k, across, t).astype(BF16)
        far(k, t, pair[k].at[across, t]).start()
        pair[k][ahead, t] = term(k, ahead, t).astype(BF16)
        two(k, t, pair[k].at[ahead, t]).start()

    def pass_square(k, t):
        mine = term(k, behind, t)
        far(k, t, pair[k].at[across, t]).wait_recv()
        far_in[k][t] = (far_in[k][t].astype(F32) + mine).astype(BF16)
        one(k, t, far_in[k].at[t]).start()

    def close_square(k, t):
        mine = term(k, p, t)
        two(k, t, pair[k].at[ahead, t]).wait_recv()
        mine = mine + two_in[k][t].astype(F32)
        one(k, t, far_in[k].at[t]).wait_recv()
        return mine + one_in[k][t].astype(F32)

    def column(k, t):
        mine = close_square(k, t)

        @pl.when((t > z) & (z > 0))
        def _():
            rise(k, t, one_in[k].at[t]).wait_recv()

        @pl.when((t < z) & (z < LINE - 1))
        def _():
            sink(k, t, one_in[k].at[t]).wait_recv()

        @pl.when(((t > z) & (z == 0)) | ((t < z) & (z == LINE - 1)))
        def _():
            one_in[k][t] = mine.astype(BF16)

        @pl.when((t > z) & (z > 0))
        def _():
            one_in[k][t] = (mine + up_in[k][t].astype(F32)).astype(BF16)

        @pl.when((t < z) & (z < LINE - 1))
        def _():
            one_in[k][t] = (mine + down_in[k][t].astype(F32)).astype(BF16)

        pl.when(t > z)(lambda: rise(k, t, one_in[k].at[t]).start())
        pl.when(t < z)(lambda: sink(k, t, one_in[k].at[t]).start())

    def finish(k):
        out[k][...] = close_square(k, z)

        @pl.when(z > 0)
        def _():
            rise(k, z, one_in[k].at[z]).wait_recv()
            out[k][...] += up_in[k][z].astype(F32)

        @pl.when(z < LINE - 1)
        def _():
            sink(k, z, one_in[k].at[z]).wait_recv()
            out[k][...] += down_in[k][z].astype(F32)

    for k in range(count):
        open_square(k, order[0])

    code = order[0] + 4 * order[1] + 16 * order[2] + 64 * order[3]

    def at(i):
        return (code // jnp.where(i == 0, 1, jnp.where(i == 1, 4, jnp.where(i == 2, 16, 64)))) % 4

    def step(i, _):
        for k in range(count):
            open_square(k, at(i + 1))
            pass_square(k, at(i))
        for k in range(count):
            column(k, at(i))
        return 0

    lax.fori_loop(0, LINE - 1, step, 0)
    for k in range(count):
        pass_square(k, z)
    for k in range(count):
        finish(k)

    def drain(i, _):
        q, t = i // LINE, i % LINE
        for k in range(count):
            to_pair(k, q, t).wait_send()
        return 0

    lax.fori_loop(0, CHIPS, drain, 0)

    def drain_line(t, _):
        for k in range(count):
            src = one_in[k].at[t]
            far(k, t, src).wait_send()
            one(k, t, src).wait_send()
            two(k, t, src).wait_send()
            pl.when(t > z)(lambda: rise(k, t, src).wait_send())
            pl.when(t < z)(lambda: sink(k, t, src).wait_send())
        return 0

    lax.fori_loop(0, LINE, drain_line, 0)


def grid_scatter(parts, collective_id):
    count = len(parts)
    slots = lambda *n: [pltpu.VMEM(n + p.shape[1:], BF16) for p in parts]
    dma = lambda *n: pltpu.SemaphoreType.DMA((count,) + n)
    return pl.pallas_call(
        functools.partial(scatter_kernel, count),
        out_shape=[jax.ShapeDtypeStruct(p.shape[1:], F32) for p in parts],
        in_specs=[pl.BlockSpec(memory_space=pl.ANY)] * count,
        out_specs=[pl.BlockSpec(memory_space=pltpu.VMEM)] * count,
        scratch_shapes=slots(SQUARE, LINE) * 2 + slots(LINE) * 5 + [dma(SQUARE, LINE)] * 3 + [dma(LINE)] * 10,
        compiler_params=pltpu.CompilerParams(
            collective_id=collective_id, has_side_effects=True, vmem_limit_bytes=60 * 2**20
        ),
        name="grid_scatter",
    )(*parts)


def on_grid():
    return lax.axis_size("seq") == 2 and lax.axis_size("dp") == CHIPS


def gather_all(parts, collective_id):
    if on_grid():
        full = grid_gather(parts, collective_id)
        return [f.reshape((-1,) + f.shape[2:]) for f in full]
    return [lax.all_gather(p, BOTH, axis=0, tiled=True) for p in parts]


def scatter_all(parts, collective_id):
    if on_grid():
        split = [p.astype(BF16).reshape(2 * CHIPS, -1, p.shape[1]) for p in parts]
        return grid_scatter(split, collective_id)
    return [lax.psum_scatter(p.astype(BF16), BOTH, scatter_dimension=0, tiled=True).astype(F32) for p in parts]


def dot(a, b):
    return jnp.dot(a, b, preferred_element_type=F32)


def dot_t(a, b):
    return lax.dot_general(a, b, (((1,), (1,)), ((), ())), preferred_element_type=F32)


def t_dot(a, b):
    return lax.dot_general(a, b, (((0,), (0,)), ((), ())), preferred_element_type=F32)


def norm_parts(v):
    center = v - jnp.mean(v, axis=-1, keepdims=True)
    inv = lax.rsqrt(jnp.mean(center * center, axis=-1, keepdims=True) + EPS)
    return center * inv, inv


def norm_grad(grad, unit, inv, gain):
    g = grad * gain
    mean_g = jnp.mean(g, axis=-1, keepdims=True)
    mean_gu = jnp.mean(g * unit, axis=-1, keepdims=True)
    return inv * (g - mean_g - unit * mean_gu)


BLOCK = 256


def head_lanes(v, a):
    lane = lax.broadcasted_iota(jnp.int32, v.shape, 1)
    return jnp.where(lane // HEAD_DIM == a, v, jnp.zeros_like(v))


def row_plans(rows, blocks, total, first):
    if blocks == 1:
        return [(0, rows, [(0, 0, total, True)])]
    if first:
        return [(0, rows, [(0, 0, rows, True)])]
    plans = []
    for r0 in range(0, rows, BLOCK):
        parts = [(1, 0, rows, False)]
        if r0:
            parts.append((0, 0, r0, False))
        plans.append((r0, BLOCK, parts + [(0, r0, BLOCK, True)]))
    return plans


def key_plans(rows, blocks, total, first):
    if blocks == 1:
        return [(0, 0, total, 0, rows, True)]
    if first:
        return [(0, k0, BLOCK, 0, rows, True) for k0 in range(0, rows, BLOCK)]
    plans = [(1, k0, BLOCK, 0, rows, False) for k0 in range(0, rows, BLOCK)]
    return plans + [(0, k0, BLOCK, k0, rows - k0, True) for k0 in range(0, rows, BLOCK)]


def by_half(blocks, run):
    if blocks == 1:
        run(False)
    else:
        pl.when(lax.axis_index("seq") == 0)(lambda: run(True))
        pl.when(lax.axis_index("seq") != 0)(lambda: run(False))


def allowed_of(own_first, k0, keys, r0, rows, first_pos, prefix_len, key_axis):
    shape = (keys, rows) if key_axis == 0 else (rows, keys)
    key_base = first_pos if own_first else 0
    key_at = key_base + k0 + lax.broadcasted_iota(jnp.int32, shape, key_axis)
    row_at = first_pos + r0 + lax.broadcasted_iota(jnp.int32, shape, 1 - key_axis)
    return key_at <= jnp.maximum(row_at, prefix_len - 1)


def forward_kernel(blocks, prefix_ref, q_ref, *refs):
    k_refs, v_refs, (o_ref, lse_ref) = refs[:blocks], refs[blocks : 2 * blocks], refs[2 * blocks :]
    rows, total = q_ref.shape[1], k_refs[0].shape[1]
    prefix_len = prefix_ref[pl.program_id(0)]
    first_pos = lax.axis_index("seq") * rows
    own_first = blocks == 2

    def run(first):
        for r0, n, parts in row_plans(rows, blocks, total, first):
            q = q_ref[0, r0 : r0 + n] * jnp.asarray(HEAD_DIM**-0.5, BF16)
            mixed = jnp.zeros((n, 2 * HEAD_DIM), F32)
            logs = jnp.zeros((n, 2 * HEAD_DIM), F32)
            lane = lax.broadcasted_iota(jnp.int32, mixed.shape, 1)
            for a in range(2):
                q_a = head_lanes(q, a)
                scores = []
                for b, k0, keys, masked in parts:
                    s = dot_t(q_a, k_refs[b][0, k0 : k0 + keys])
                    if masked:
                        ok = allowed_of(own_first, k0, keys, r0, n, first_pos, prefix_len, 1)
                        s = jnp.where(ok, s, -1e30)
                    scores.append(s)
                top = functools.reduce(jnp.maximum, [jnp.max(s, axis=1, keepdims=True) for s in scores])
                total_exp = jnp.zeros_like(top)
                out = jnp.zeros_like(mixed)
                for s, (b, k0, keys, _) in zip(scores, parts):
                    p = jnp.exp(s - top)
                    total_exp = total_exp + jnp.sum(p, axis=1, keepdims=True)
                    out = out + dot(p.astype(BF16), v_refs[b][0, k0 : k0 + keys])
                mine = lane // HEAD_DIM == a
                mixed = jnp.where(mine, out / total_exp, mixed)
                logs = jnp.where(mine, top + jnp.log(total_exp), logs)
            o_ref[0, r0 : r0 + n] = mixed.astype(BF16)
            logs = logs.T
            lse_ref[0, 0, 0:1, r0 : r0 + n] = logs[0:1]
            lse_ref[0, 0, 1:2, r0 : r0 + n] = logs[HEAD_DIM : HEAD_DIM + 1]

    by_half(blocks, run)


def backward_kernel(blocks, prefix_ref, q_ref, o_ref, lse_ref, g_ref, *refs):
    k_refs, v_refs, gq_ref = refs[:blocks], refs[blocks : 2 * blocks], refs[2 * blocks]
    gk_refs, gv_refs = refs[2 * blocks + 1 : 3 * blocks + 1], refs[3 * blocks + 1 : 4 * blocks + 1]
    dots, acc = refs[4 * blocks + 1 :]
    rows, total = q_ref.shape[1], k_refs[0].shape[1]
    prefix_len = prefix_ref[pl.program_id(0)]
    first_pos = lax.axis_index("seq") * rows
    own_first = blocks == 2
    scale = HEAD_DIM**-0.5
    product = (g_ref[0].astype(F32) * o_ref[0].astype(F32)).T
    for a in range(2):
        dots[a : a + 1] = jnp.sum(product[a * HEAD_DIM : (a + 1) * HEAD_DIM], axis=0, keepdims=True)
    acc[...] = jnp.zeros_like(acc)

    def run(first):
        for b, k0, keys, r0, n, masked in key_plans(rows, blocks, total, first):
            k = k_refs[b][0, k0 : k0 + keys]
            v = v_refs[b][0, k0 : k0 + keys]
            q = q_ref[0, r0 : r0 + n] * jnp.asarray(scale, BF16)
            g = g_ref[0, r0 : r0 + n]
            gk = jnp.zeros((keys, 2 * HEAD_DIM), F32)
            gv = jnp.zeros((keys, 2 * HEAD_DIM), F32)
            gq = jnp.zeros((n, 2 * HEAD_DIM), F32)
            for a in range(2):
                q_a, g_a = head_lanes(q, a), head_lanes(g, a)
                s = dot_t(k, q_a)
                if masked:
                    ok = allowed_of(own_first, k0, keys, r0, n, first_pos, prefix_len, 0)
                    s = jnp.where(ok, s, -1e30)
                p = jnp.exp(s - lse_ref[0, 0, a : a + 1, r0 : r0 + n])
                gv = gv + dot(p.astype(BF16), g_a)
                grad_p = dot_t(v, g_a)
                grad_s = (p * (grad_p - dots[a : a + 1, r0 : r0 + n])).astype(BF16)
                gk = gk + dot(grad_s, q_a)
                gq = gq + t_dot(grad_s, head_lanes(k, a))
            gk_refs[b][0, k0 : k0 + keys] = gk.astype(BF16)
            gv_refs[b][0, k0 : k0 + keys] = gv.astype(BF16)
            acc[r0 : r0 + n] = acc[r0 : r0 + n] + gq
        if first:
            gk_refs[1][...] = jnp.zeros_like(gk_refs[1])
            gv_refs[1][...] = jnp.zeros_like(gv_refs[1])

    by_half(blocks, run)
    gq_ref[0] = (acc[...] * scale).astype(BF16)


def pair_spec(length):
    return pl.BlockSpec((1, length, 2 * HEAD_DIM), lambda m, h, prefix: (m, 0, h))


def attention(q, keys, values, prefix):
    micros, rows, width = q.shape
    blocks, total = len(keys), keys[0].shape[1]
    pairs = HEADS // 2
    return pl.pallas_call(
        functools.partial(forward_kernel, blocks),
        out_shape=[
            jax.ShapeDtypeStruct(q.shape, BF16),
            jax.ShapeDtypeStruct((micros, pairs, 8, rows), F32),
        ],
        grid_spec=pltpu.PrefetchScalarGridSpec(
            num_scalar_prefetch=1,
            grid=(micros, pairs),
            in_specs=[pair_spec(rows)] + [pair_spec(total)] * (2 * blocks),
            out_specs=[pair_spec(rows), pl.BlockSpec((1, 1, 8, rows), lambda m, h, prefix: (m, h, 0, 0))],
        ),
        compiler_params=pltpu.CompilerParams(vmem_limit_bytes=48 * 2**20),
        cost_estimate=pl.CostEstimate(
            flops=8 * micros * rows * blocks * total * width,
            bytes_accessed=4 * micros * (rows + blocks * total) * width,
            transcendentals=micros * rows * blocks * total * HEADS,
        ),
        name="attention_forward",
    )(prefix, q, *keys, *values)


def attention_back(q, keys, values, mixed, lse, grad, prefix):
    micros, rows, width = q.shape
    blocks, total = len(keys), keys[0].shape[1]
    pairs = HEADS // 2
    grads = pl.pallas_call(
        functools.partial(backward_kernel, blocks),
        out_shape=[jax.ShapeDtypeStruct(t.shape, BF16) for t in (q, *keys, *values)],
        grid_spec=pltpu.PrefetchScalarGridSpec(
            num_scalar_prefetch=1,
            grid=(micros, pairs),
            in_specs=[
                pair_spec(rows),
                pair_spec(rows),
                pl.BlockSpec((1, 1, 8, rows), lambda m, h, prefix: (m, h, 0, 0)),
                pair_spec(rows),
            ]
            + [pair_spec(total)] * (2 * blocks),
            out_specs=[pair_spec(rows)] + [pair_spec(total)] * (2 * blocks),
            scratch_shapes=[pltpu.VMEM((8, rows), F32), pltpu.VMEM((rows, 2 * HEAD_DIM), F32)],
        ),
        compiler_params=pltpu.CompilerParams(vmem_limit_bytes=48 * 2**20),
        cost_estimate=pl.CostEstimate(
            flops=20 * micros * rows * blocks * total * width,
            bytes_accessed=8 * micros * (rows + blocks * total) * width,
            transcendentals=micros * rows * blocks * total * HEADS,
        ),
        name="attention_backward",
    )(prefix, q, mixed, lse, grad, *keys, *values)
    return grads[0], grads[1 : 1 + blocks], grads[1 + blocks :]


def on_device(
    inputs,
    query_weight,
    key_weight,
    value_weight,
    query_bias,
    value_bias,
    output_weight,
    output_bias,
    first_gain,
    first_shift,
    inner_weight,
    inner_bias,
    outer_weight,
    outer_bias,
    second_gain,
    second_shift,
    prefix,
    cotangent,
):
    micros, rows, width = inputs.shape[1:]
    own = query_weight.shape[0]
    hidden_width = inner_weight.shape[1]
    per = hidden_width // width
    seqs = lax.axis_size("seq")
    x = inputs[0]
    flat_x = x.reshape(micros * rows, width)

    if seqs == 2:
        before = lax.ppermute(x, "seq", [(0, 1)])
        key_x = [flat_x, before.reshape(micros * rows, width)]
    else:
        key_x = [lax.all_gather(x, "seq", axis=1, tiled=True).reshape(-1, width)]

    vectors = (query_bias, value_bias, output_bias, first_gain, first_shift, outer_bias, second_gain, second_shift)
    small = jnp.concatenate([jnp.stack(vectors, axis=1), inner_bias.reshape(own, per)], axis=1)
    small_count = small.shape[1]
    small = jnp.pad(small, ((0, 0), (0, 128 - small_count)))
    full = gather_all(
        [query_weight, key_weight, value_weight, small, output_weight, inner_weight, outer_weight], 1
    )
    full_query, full_key, full_value, small_all, full_output, full_inner, full_outer = full
    small_all = small_all[:, :small_count].astype(F32)
    qb, vb, ob, fg, fs, ub, sg, ss = [small_all[:, i] for i in range(8)]
    ib = small_all[:, 8:].reshape(hidden_width)

    queries = (dot(flat_x, full_query) + qb).astype(BF16).reshape(micros, rows, width)
    keys = [dot(t, full_key).astype(BF16).reshape(micros, -1, width) for t in key_x]
    values = [(dot(t, full_value) + vb).astype(BF16).reshape(micros, -1, width) for t in key_x]

    mixed_parts, lse = attention(queries, keys, values, prefix[0])
    mixed = mixed_parts.reshape(micros * rows, width)

    unit1, inv1 = norm_parts(flat_x.astype(F32) + dot(mixed, full_output) + ob)
    middle = unit1 * fg + fs
    middle_low = middle.astype(BF16)
    inner = dot(middle_low, full_inner) + ib
    half_cdf = 0.5 * (1.0 + lax.erf(inner * (0.5**0.5)))
    hidden = (inner * half_cdf).astype(BF16)
    slope = half_cdf + inner * jnp.exp(-0.5 * inner * inner) * 0.3989422804014327
    unit2, inv2 = norm_parts(middle + dot(hidden, full_outer) + ub)
    result = (unit2 * sg + ss).astype(BF16)

    cot = cotangent[0].reshape(micros * rows, width).astype(F32)
    g_sgain = jnp.sum(cot * unit2, axis=0)
    g_sshift = jnp.sum(cot, axis=0)
    grad_mid2 = norm_grad(cot, unit2, inv2, sg)
    grad_outer = grad_mid2.astype(BF16)
    g_ubias = jnp.sum(grad_outer.astype(F32), axis=0)
    g_outer = t_dot(hidden, grad_outer).astype(BF16)
    grad_hidden = dot_t(grad_outer, full_outer).astype(BF16)
    grad_inner = (grad_hidden.astype(F32) * slope).astype(BF16)
    g_ibias = jnp.sum(grad_inner.astype(F32), axis=0)
    g_inner = t_dot(middle_low, grad_inner)
    grad_middle = grad_mid2 + dot_t(grad_inner, full_inner)
    g_fgain = jnp.sum(grad_middle * unit1, axis=0)
    g_fshift = jnp.sum(grad_middle, axis=0)
    grad_sum1 = norm_grad(grad_middle, unit1, inv1, fg)
    grad_branch = grad_sum1.astype(BF16)
    g_obias = jnp.sum(grad_branch.astype(F32), axis=0)
    g_output = t_dot(mixed, grad_branch)
    grad_mixed = dot_t(grad_branch, full_output).astype(BF16).reshape(micros, rows, width)

    grad_q, grad_k, grad_v = attention_back(
        queries, keys, values, mixed_parts, lse, grad_mixed, prefix[0]
    )
    grad_q = grad_q.reshape(micros * rows, width)
    grad_k = [t.reshape(-1, width) for t in grad_k]
    grad_v = [t.reshape(-1, width) for t in grad_v]
    g_qbias = jnp.sum(grad_q.astype(F32), axis=0)
    g_vbias = sum(jnp.sum(t.astype(F32), axis=0) for t in grad_v)
    g_query = t_dot(flat_x, grad_q)
    g_key = sum(t_dot(t, g) for t, g in zip(key_x, grad_k))
    g_value = sum(t_dot(t, g) for t, g in zip(key_x, grad_v))
    g_small = jnp.concatenate(
        [
            jnp.stack([g_qbias, g_vbias, g_obias, g_fgain, g_fshift, g_ubias, g_sgain, g_sshift], axis=1),
            g_ibias.reshape(width, per),
        ],
        axis=1,
    )
    g_small = jnp.pad(g_small, ((0, 0), (0, 128 - small_count)))
    own_grads = scatter_all([g_outer, g_inner, g_output, g_query, g_key, g_value, g_small], 3)
    own_outer, own_inner, own_output, own_query, own_key, own_value, own_small = own_grads

    via_kv = [dot_t(k, full_key) + dot_t(v, full_value) for k, v in zip(grad_k, grad_v)]
    via_kv = [t.reshape(micros, -1, width) for t in via_kv]
    grad_x = (grad_sum1 + dot_t(grad_q, full_query)).reshape(micros, rows, width)
    if seqs == 2:
        grad_x = grad_x + via_kv[0]
        grad_x = grad_x + lax.ppermute(via_kv[1].astype(BF16), "seq", [(1, 0)]).astype(F32)
    else:
        grad_x = grad_x + lax.psum_scatter(via_kv[0], "seq", scatter_dimension=1, tiled=True)

    vec = own_small[:, :small_count]
    v_of = [vec[:, i] for i in range(8)]
    outputs = result.reshape(micros, rows, width)[None]
    return (
        outputs,
        grad_x[None],
        own_query,
        own_key,
        own_value,
        v_of[0],
        v_of[1],
        own_output,
        v_of[2],
        v_of[3],
        v_of[4],
        own_inner,
        vec[:, 8:].reshape(own * per),
        own_outer,
        v_of[5],
        v_of[6],
        v_of[7],
    )


def solution(mesh):
    act = P("dp", None, "seq", None)
    mat = P(BOTH, None)
    vec = P(BOTH)
    params = (mat, mat, mat, vec, vec, mat, vec, vec, vec, mat, vec, mat, vec, vec, vec)
    return jax.shard_map(
        on_device,
        mesh=mesh,
        in_specs=(act,) + params + (P("dp", None), act),
        out_specs=(act, act) + params,
        check_vma=False,
    )
```

profile of v0, /device:TPU:12, one launch (start us, length us, event | category | flops | bytes accessed | tf_op | source)
XLA Modules:
  0.0 421.5 jit_solution(3347003924281930421)
XLA Ops:
  0.8 2.7 copy.85
  6.4 98.9 %grid_gather.1 = (bf16[32,24,768]{2,1,0:T(8,128)(2,1)}, bf16[32,24,768]{2,1,0:T(8,128)(2,1)}, bf16[32,24,768]{2,1,0:T(8,128)(2,1)}, bf16[32,24,128]{2,1,0:T(8,12...) custom-call(bf16[24,768]{1,0:T(8,128)(2,1)} %refs_0_.1, ...), custom_call_target="tpu_custom_call" | custom-call | tf_op jit(solution)/shard_map/grid_gather/pallas_call | solution.py:172
  106.9 3.9 fusion.18
  112.6 4.4 %fusion.16 = bf16[1024,768]{0,1:T(8,128)(2,1)} fusion(bf16[768,768]{1,0:T(8,128)(2,1)} %bitcast.193, bf16[1024,768]{1,0:T(8,128)(2,1)S(1)} %bitcast.150), kind=kOutput, calls=%fused_computation.52 | convolution fusion | flops 1208745984 | bytes 4325376 | tf_op jit(solution)/shard_map/dot_general | solution.py:370
  118.8 5.0 %fusion.19 = bf16[1024,768]{0,1:T(8,128)(2,1)} fusion(f32[768]{0:T(1024)S(1)} %get-tuple-element.71, bf16[768,768]{1,0:T(8,128)(2,1)} %bitcast.168, bf16[1024,768]{1,0:T(8,128)(2,1)} %bitcast.147), kind=kOutput, calls=%fused_computation.55 | convolution fusion | flops 1209532416 | bytes 4328448 | tf_op jit(solution)/shard_map/dot_general | solution.py:370
  132.5 4.5 %fusion.17 = bf16[1024,768]{0,1:T(8,128)(2,1)} fusion(bf16[768,768]{1,0:T(8,128)(2,1)} %bitcast.194, bf16[1024,768]{1,0:T(8,128)(2,1)} %bitcast.161), kind=kOutput, calls=%fused_computation.53 | convolution fusion | flops 1208745984 | bytes 4325376 | tf_op jit(solution)/shard_map/dot_general | solution.py:370
  145.0 28.2 %attention_forward.1 = (bf16[2,512,768]{2,1,0:T(8,128)(2,1)S(1)}, f32[2,6,8,512]{3,2,1,0:T(8,128)S(1)}) custom-call(s32[2]{0:T(128)S(1)} %bitcast.135, bf16[2,512,768]{2,1,0:T(8,128)(2,1)S(1)} %bitcast.129, bf16[2,512,768]{2,1,0:T(8,128)(2,1)S(1)} %bitcast.131, bf16[2,512,768]{2,1,0:T(8,128)(2,1)} %bitcast.156, bf16[2,512,768]{2,1,0:T(8,128)(2,1)} %bitcast.154, ...), custom_call_target="tpu_custom_call" | custom-call | flops 6442450944 | bytes 9437184 | tf_op jit(solution)/shard_map/attention_forward/pallas_call | solution.py:535
  176.1 9.1 %multiply_convert_fusion = (bf16[1024,3072]{1,0:T(8,128)(2,1)S(1)}, f32[1024,3072]{1,0:T(8,128)}) fusion(f32[3072]{0:T(1024)S(1)} %add.171, bf16[768,3072]{1,0:T(8,128)(2,1)S(1)} %bitcast.185, f32[1024,768]{1,0:T(8,128)S(1)} %get-tuple-element.87, f32[768]{0:T(1024)S(1)} %get-tuple-element.68, f32[768]{0:T(1024)S(1)} %get-tuple-element.69, ...), kind=kOutput, calls=%fused_computation.7 | convolution fusion | flops 4854644736 | bytes 26765312 | tf_op jit(solution)/shard_map/dot_general | solution.py:370
  185.2 5.5 %fusion.30 = (f32[1024]{0:T(1024)S(1)}, f32[1024,768]{1,0:T(8,128)S(1)}) fusion(f32[768]{0:T(1024)S(1)} %get-tuple-element.67, bf16[1024,3072]{1,0:T(8,128)(2,1)S(1)} %get-tuple-element.88, bf16[3072,768]{1,0:T(8,128)(2,1)S(1)} %bitcast.189, f32[768]{0:T(1024)S(1)} %get-tuple-element.68, f32[768]{0:T(1024)S(1)} %get-tuple-element.69, ...), kind=kOutput, calls=%fused_computation.90 | convolution fusion | flops 4837342208 | bytes 17323008 | tf_op jit(solution)/shard_map/dot_general | solution.py:370
  192.0 2.7 fusion.12
  196.1 7.1 %convolution_convert_fusion.1 = bf16[3072,768]{1,0:T(8,128)(2,1)} fusion(bf16[1024,3072]{1,0:T(8,128)(2,1)S(1)} %get-tuple-element.88, f32[1024,768]{1,0:T(8,128)S(1)} %get-tuple-element.82), kind=kOutput, calls=%fused_computation.10 | convolution fusion | flops 4834983936 | bytes 14155776 | tf_op jit(solution)/shard_map/dot_general | solution.py:378
  203.2 13.1 %fusion.31 = (bf16[3072]{0:T(1024)(128)(2,1)S(1)}, bf16[1024,3072]{1,0:T(8,128)(2,1)}) fusion(f32[1024,3072]{1,0:T(8,128)} %get-tuple-element.89, f32[3072]{0:T(1024)S(1)} %add.171, bf16[3072,768]{1,0:T(8,128)(2,1)S(1)} %bitcast.190, f32[1024,768]{1,0:T(8,128)S(1)} %get-tuple-element.82), kind=kOutput, calls=%fused_computation.91 | convolution fusion | flops 4876661760 | bytes 26757120 | tf_op jit(solution)/shard_map/dot_general | solution.py:374
  216.2 8.1 %multiply_reduce_fusion = (bf16[768]{0:T(1024)(128)(2,1)S(1)}, f32[1024]{0:T(1024)S(1)}, f32[1024]{0:T(1024)S(1)}, bf16[768]{0:T(1024)(128)(2,1)S(1)}, f32[1024,768]{1,0:T(8,128)S(1)}) fusion(f32[1024,768]{1,0:T(8,128)S(1)} %get-tuple-element.87, f32[1024]{0:T(1024)S(1)} %add_rsqrt_fusion.1, f32[1024]{0:T(1024)S(1)} %broadcast_multiply_fusion.4, ...), kind=kOutput, calls=%fused_computation.21 | convolution fusion | flops 4839698432 | bytes 20469760 | tf_op jit(solution)/shard_map/dot_general | solution.py:374
  224.4 9.9 %convolution_convert_fusion = bf16[768,3072]{1,0:T(8,128)(2,1)} fusion(bf16[1024,3072]{1,0:T(8,128)(2,1)} %get-tuple-element.94, f32[1024,768]{1,0:T(8,128)S(1)} %get-tuple-element.87, f32[768]{0:T(1024)S(1)} %get-tuple-element.68, f32[768]{0:T(1024)S(1)} %get-tuple-element.69, f32[1024]{0:T(1024)S(1)} %add_rsqrt_fusion.1, f32[1024]{0:T(1024)S(1)} %broadcast_multiply_fusion.4), kind=kOutput, calls=%fused_computation.9 | convolution fusion | flops 4838129664 | bytes 14170112 | tf_op jit(solution)/shard_map/dot_general | solution.py:378
  240.7 44.9 %attention_backward.1 = (bf16[2,512,768]{2,1,0:T(8,128)(2,1)S(1)}, bf16[2,512,768]{2,1,0:T(8,128)(2,1)S(1)}, bf16[2,512,768]{2,1,0:T(8,128)(2,1)S(1)}, bf16[2,512,768]{2,1,0:T(8,128)(2,1)}, bf16[2,512,768]{2,1,0:T(8,128)(2,1)}) custom-call(s32[2]{0:T(128)S(1)} %bitcast.136, bf16[2,512,768]{2,1,0:T(8,128)(2,1)} %bitcast.130, bf16[2,512,768]{2,1,0:T(8,128)(2,1)} %copy-done.3, ...), custom_call_target="tpu_custom_call" | custom-call | flops 16106127360 | bytes 18874368 | tf_op jit(solution)/shard_map/attention_backward/pallas_call | solution.py:561
  290.4 2.9 collective-permute-start.1
  293.6 4.1 convolution_convert_fusion.5
  297.6 2.9 fusion.35
  300.9 2.9 fusion.36
  305.4 5.2 %fusion.15 = bf16[768,768]{0,1:T(8,128)(2,1)} fusion(f32[768,768]{0,1:T(8,128)} %fusion.35, bf16[2,512,768]{1,2,0:T(8,128)(2,1)} %collective-permute-done, bf16[2,512,768]{2,1,0:T(8,128)(2,1)} %copy-done.4), kind=kOutput, calls=%fused_computation.45 | convolution fusion | flops 1209139200 | bytes 6684672 | tf_op jit(solution)/shard_map/dot_general | solution.py:378
  310.6 3.8 fusion.14
  314.4 89.3 %grid_scatter.1 = (f32[96,768]{1,0:T(8,128)}, f32[24,3072]{1,0:T(8,128)}, f32[24,768]{1,0:T(8,128)}, f32[24,768]{1,0:T(8,128)}, f32[24,768]{1,0:T(8,128)}, /*index=5*/f32[24,768]{1,0:T(8,128)}, f32[24,128]{1,0:T(8,128)}) custom-call(bf16[32,96,768]{2,1,0:T(8,128)(2,1)} %bitcast.145, bf16[32,24,3072]{2,1,0:T(8,128)(2,1)} %bitcast.146, ...), custom_call_target="tpu_custom_call" | custom-call | tf_op jit(solution)/shard_map/grid_scatter/pallas_call | solution.py:338
  406.9 2.8 fusion.33
  413.9 3.5 add_bitcast_fusion
  (160 shorter events, 54.8 us)
Async XLA Ops:
  0.7 106.2 %copy-start.10 = (bf16[1,2,512,768]{3,2,1,0:T(8,128)(2,1)S(1)}, bf16[1,2,512,768]{3,2,1,0:T(8,128)(2,1)}, u32[]{:S(2)}) copy-start(bf16[1,2,512,768]{3,2,1,0:T(8,128)(2,1)} %param.18) | copy-start | bytes 4718596
  0.7 4.5 %copy-start.30 = (bf16[24]{0:T(256)(128)(2,1)S(1)}, bf16[24]{0:T(256)(128)(2,1)}, u32[]{:S(2)}) copy-start(bf16[24]{0:T(256)(128)(2,1)} %param.31) | copy-start | bytes 148
  0.7 4.6 %copy-start.31 = (bf16[24]{0:T(256)(128)(2,1)S(1)}, bf16[24]{0:T(256)(128)(2,1)}, u32[]{:S(2)}) copy-start(bf16[24]{0:T(256)(128)(2,1)} %param.32) | copy-start | bytes 148
  0.7 4.7 %copy-start.32 = (bf16[24]{0:T(256)(128)(2,1)S(1)}, bf16[24]{0:T(256)(128)(2,1)}, u32[]{:S(2)}) copy-start(bf16[24]{0:T(256)(128)(2,1)} %param.33) | copy-start | bytes 148
  0.8 4.8 %copy-start.33 = (bf16[96]{0:T(256)(128)(2,1)S(1)}, bf16[96]{0:T(256)(128)(2,1)}, u32[]{:S(2)}) copy-start(bf16[96]{0:T(256)(128)(2,1)} %param.29) | copy-start | bytes 580
  3.4 126.4 %collective-permute-start = (bf16[2,512,768]{1,2,0:T(8,128)(2,1)}, bf16[2,512,768]{1,2,0:T(8,128)(2,1)}, u32[]{:S(2)}, u32[]{:S(2)}) collective-permute-start(bf16[2,512,768]{1,2,0:T(8,128)(2,1)} %bitcast.17), channel_id=1, source_target_pairs={{0,16},{1,17},{2,18},{3,19},{4,20},{5,21},{6,22},{7,23},{8,24},{9,... | collective-permute-start | bytes 4718600 | tf_op jit(solution)/shard_map/ppermute | solution.py:617
  112.6 32.4 %copy-start = (bf16[1024,768]{1,0:T(8,128)(2,1)}, bf16[1024,768]{1,0:T(8,128)(2,1)S(1)}, u32[]{:S(2)}) copy-start(bf16[1024,768]{1,0:T(8,128)(2,1)S(1)} %copy.83) | copy-start | bytes 4718596
  118.8 26.2 %copy-start.1 = (bf16[1024,768]{1,0:T(8,128)(2,1)}, bf16[1024,768]{1,0:T(8,128)(2,1)S(1)}, u32[]{:S(2)}) copy-start(bf16[1024,768]{1,0:T(8,128)(2,1)S(1)} %copy.84) | copy-start | bytes 4718596
  132.5 4.5 %copy-start.15 = (bf16[2,512,768]{2,1,0:T(8,128)(2,1)S(1)}, bf16[2,512,768]{2,1,0:T(8,128)(2,1)}, u32[]{:S(2)}) copy-start(bf16[2,512,768]{2,1,0:T(8,128)(2,1)} %copy.86) | copy-start | bytes 4718596
  132.5 4.5 %copy-start.16 = (bf16[32,24,768]{2,1,0:T(8,128)(2,1)S(1)}, bf16[32,24,768]{2,1,0:T(8,128)(2,1)}, u32[]{:S(2)}) copy-start(bf16[32,24,768]{2,1,0:T(8,128)(2,1)} %get-tuple-element.41) | copy-start | bytes 3538948
  139.6 5.3 %copy-start.2 = (s32[1,2]{1,0:T(1,128)S(1)}, s32[1,2]{1,0:T(1,128)}, u32[]{:S(2)}) copy-start(s32[1,2]{1,0:T(1,128)} %param.34) | copy-start | bytes 28
  144.9 28.3 %copy-start.11 = (bf16[1,2,512,768]{3,2,1,0:T(8,128)(2,1)S(1)}, bf16[1,2,512,768]{3,2,1,0:T(8,128)(2,1)}, u32[]{:S(2)}) copy-start(bf16[1,2,512,768]{3,2,1,0:T(8,128)(2,1)} %param.18) | copy-start | bytes 4718596
  145.0 28.3 %copy-start.36 = (bf16[32,24,768]{2,1,0:T(8,128)(2,1)S(1)}, bf16[32,24,768]{2,1,0:T(8,128)(2,1)}, u32[]{:S(2)}) copy-start(bf16[32,24,768]{2,1,0:T(8,128)(2,1)} %get-tuple-element.43) | copy-start | bytes 3538948
  173.2 65.0 %copy-start.3 = (bf16[2,512,768]{2,1,0:T(8,128)(2,1)}, bf16[2,512,768]{2,1,0:T(8,128)(2,1)S(1)}, u32[]{:S(2)}) copy-start(bf16[2,512,768]{2,1,0:T(8,128)(2,1)S(1)} %get-tuple-element.42.o_ref) | copy-start | bytes 4718596
  174.8 10.4 %slice-start.2 = ((s8[4718592]{0:T(1024)(128)(4,1)}), s8[4194304]{0:T(1024)(128)(4,1)S(1)}, s32[]{:S(2)}) async-start(s8[4718592]{0:T(1024)(128)(4,1)} %bitcast.187), calls=%async_computation.2 | async-start | bytes 8388608
  176.1 9.1 %slice-start.3 = ((s8[4718592]{0:T(1024)(128)(4,1)}), s8[524288]{0:T(1024)(128)(4,1)S(1)}, s32[]{:S(2)}) async-start(s8[4718592]{0:T(1024)(128)(4,1)} %bitcast.187), calls=%async_computation.3 | async-start | bytes 1048576
  240.7 44.9 %copy-start.35 = (bf16[32,24,768]{2,1,0:T(8,128)(2,1)S(1)}, bf16[32,24,768]{2,1,0:T(8,128)(2,1)}, u32[]{:S(2)}) copy-start(bf16[32,24,768]{2,1,0:T(8,128)(2,1)} %get-tuple-element.40) | copy-start | bytes 3538948
  290.4 123.5 %collective-permute-start.1 = (bf16[2,512,768]{2,1,0:T(8,128)(2,1)}, bf16[2,512,768]{2,1,0:T(8,128)(2,1)}, u32[]{:S(2)}, u32[]{:S(2)}) collective-permute-start(bf16[2,512,768]{2,1,0:T(8,128)(2,1)} %bitcast.39), channel_id=1, source_target_pairs={{16,0},{17,1},{18,2},{19,3},{20,4},{21,5},{22,6},{23,7},{24,8},{25... | collective-permute-start | bytes 4718600 | tf_op jit(solution)/shard_map/ppermute | solution.py:698
  305.4 5.2 %copy-start.14 = (bf16[2,512,768]{2,1,0:T(8,128)(2,1)S(1)}, bf16[2,512,768]{2,1,0:T(8,128)(2,1)}, u32[]{:S(2)}) copy-start(bf16[2,512,768]{2,1,0:T(8,128)(2,1)} %get-tuple-element.51) | copy-start | bytes 4718596
  305.4 5.2 %copy-start.37 = (f32[768,768]{0,1:T(8,128)S(1)}, f32[768,768]{0,1:T(8,128)}, u32[]{:S(2)}) copy-start(f32[768,768]{0,1:T(8,128)} %fusion.36) | copy-start | bytes 7077892
  413.9 4.8 %copy-start.22 = (f32[24,768]{1,0:T(8,128)S(1)}, f32[24,768]{1,0:T(8,128)}, u32[]{:S(2)}) copy-start(f32[24,768]{1,0:T(8,128)} %get-tuple-element.118) | copy-start | bytes 221188
  413.9 5.4 %copy-start.21 = (f32[24,768]{1,0:T(8,128)S(1)}, f32[24,768]{1,0:T(8,128)}, u32[]{:S(2)}) copy-start(f32[24,768]{1,0:T(8,128)} %get-tuple-element.121) | copy-start | bytes 221188
  413.9 6.0 %copy-start.20 = (f32[24,3072]{1,0:T(8,128)S(1)}, f32[24,3072]{1,0:T(8,128)}, u32[]{:S(2)}) copy-start(f32[24,3072]{1,0:T(8,128)} %get-tuple-element.125) | copy-start | bytes 884740
  413.9 6.7 %copy-start.19 = (f32[96,768]{1,0:T(8,128)S(1)}, f32[96,768]{1,0:T(8,128)}, u32[]{:S(2)}) copy-start(f32[96,768]{1,0:T(8,128)} %get-tuple-element.127) | copy-start | bytes 884740
  (20 other events, 61.0 us)
where the time goes:
time: 425 us; the launch traced here: 422 us
  Pallas kernels  261 us (61%)
  matrix products  108 us (25%)
  local copies, waits for them, and re-layouts  32.1 us (8%)
  other arithmetic  14.3 us (3%)
    pallas_call x1, Pallas kernels, grid_gather(): pl.pallas_call(functools.partial(gather_kernel, count), out_shape=[jax.Sh...  98.9 us
    pallas_call x1, Pallas kernels, grid_scatter(): pl.pallas_call(functools.partial(scatter_kernel, count), out_shape=[jax.S...  89.3 us
    pallas_call x1, Pallas kernels, attention_back(): pl.pallas_call(functools.partial(backward_kernel, blocks), out_shape=[jax...  44.9 us
    dot_general x8, matrix products, t_dot(): lax.dot_general(a, b, (((0,), (0,)), ((), ())), preferred_element_type=F32)  38.4 us
    dot_general x8, matrix products, dot(): return jnp.dot(a, b, preferred_element_type=F32)  36.5 us
    dot_general x8, matrix products, dot_t(): lax.dot_general(a, b, (((1,), (1,)), ((), ())), preferred_element_type=F32)  33.4 us
    pallas_call x1, Pallas kernels, attention(): pl.pallas_call(functools.partial(forward_kernel, blocks), out_shape=[jax....  28.2 us
    unnamed x94, local copies, waits for them, and re-layouts  11.4 us
  transfers between devices with their start and end apart: 2, of which 0 were waited for; matrix products, arithmetic and copies ran while one was open for 13% of the time, Pallas kernels for 45%

commit v1 on v0

--- a/solution.py
+++ b/solution.py
@@ -585,6 +585,82 @@
     return grads[0], grads[1 : 1 + blocks], grads[1 + blocks :]
 
 
+def project_kernel(x_ref, before_ref, wq_ref, wk_ref, wv_ref, qb_ref, vb_ref, q_ref, k0_ref, k1_ref, v0_ref, v1_ref):
+    x = x_ref[...]
+    q_ref[...] = (dot(x, wq_ref[...]) + qb_ref[...]).astype(BF16)
+    for rows_in, k_ref, v_ref in ((x, k0_ref, v0_ref), (before_ref[...], k1_ref, v1_ref)):
+        k_ref[...] = dot(rows_in, wk_ref[...]).astype(BF16)
+        v_ref[...] = (dot(rows_in, wv_ref[...]) + vb_ref[...]).astype(BF16)
+
+
+def project(x, before, wq, wk, wv, qb, vb):
+    count, width = x.shape
+    rows = pl.BlockSpec((2 * BLOCK, width), lambda i: (i, 0))
+    whole = pl.BlockSpec((width, width), lambda i: (0, 0))
+    vector = pl.BlockSpec((1, width), lambda i: (0, 0))
+    return pl.pallas_call(
+        project_kernel,
+        out_shape=[jax.ShapeDtypeStruct(x.shape, BF16)] * 5,
+        grid=(count // (2 * BLOCK),),
+        in_specs=[rows, rows, whole, whole, whole, vector, vector],
+        out_specs=[rows] * 5,
+        compiler_params=pltpu.CompilerParams(vmem_limit_bytes=48 * 2**20),
+        cost_estimate=pl.CostEstimate(
+            flops=10 * count * width * width, bytes_accessed=14 * count * width + 6 * width * width, transcendentals=0
+        ),
+        name="project",
+    )(x, before, wq, wk, wv, qb[None], vb[None])
+
+
+def unproject_kernel(
+    x_ref, before_ref, sum1_ref, gq_ref, gk0_ref, gk1_ref, gv0_ref, gv1_ref, wq_ref, wk_ref, wv_ref,
+    gx_ref, via_ref, gwq_ref, gwk_ref, gwv_ref, sums_ref, acc_q, acc_k, acc_v,
+):
+    step = pl.program_id(0)
+
+    @pl.when(step == 0)
+    def _():
+        for ref in (acc_q, acc_k, acc_v, sums_ref):
+            ref[...] = jnp.zeros_like(ref)
+
+    x, before = x_ref[...], before_ref[...]
+    gq, gk0, gk1, gv0, gv1 = gq_ref[...], gk0_ref[...], gk1_ref[...], gv0_ref[...], gv1_ref[...]
+    via_ref[...] = (dot_t(gk1, wk_ref[...]) + dot_t(gv1, wv_ref[...])).astype(BF16)
+    gx_ref[...] = sum1_ref[...] + dot_t(gq, wq_ref[...]) + dot_t(gk0, wk_ref[...]) + dot_t(gv0, wv_ref[...])
+    acc_q[...] += t_dot(x, gq)
+    acc_k[...] += t_dot(x, gk0) + t_dot(before, gk1)
+    acc_v[...] += t_dot(x, gv0) + t_dot(before, gv1)
+    sums_ref[0:1] += jnp.sum(gq.astype(F32), axis=0, keepdims=True)
+    sums_ref[1:2] += jnp.sum(gv0.astype(F32) + gv1.astype(F32), axis=0, keepdims=True)
+
+    @pl.when(step == pl.num_programs(0) - 1)
+    def _():
+        gwq_ref[...] = acc_q[...].astype(BF16)
+        gwk_ref[...] = acc_k[...].astype(BF16)
+        gwv_ref[...] = acc_v[...].astype(BF16)
+
+
+def unproject(x, before, sum1, gq, gk, gv, wq, wk, wv):
+    count, width = x.shape
+    rows = pl.BlockSpec((BLOCK, width), lambda i: (i, 0))
+    whole = pl.BlockSpec((width, width), lambda i: (0, 0))
+    return pl.pallas_call(
+        unproject_kernel,
+        out_shape=[jax.ShapeDtypeStruct(x.shape, F32), jax.ShapeDtypeStruct(x.shape, BF16)]
+        + [jax.ShapeDtypeStruct(wq.shape, BF16)] * 3
+        + [jax.ShapeDtypeStruct((8, width), F32)],
+        grid=(count // BLOCK,),
+        in_specs=[rows] * 8 + [whole] * 3,
+        out_specs=[rows] * 2 + [whole] * 3 + [pl.BlockSpec((8, width), lambda i: (0, 0))],
+        scratch_shapes=[pltpu.VMEM(wq.shape, F32)] * 3,
+        compiler_params=pltpu.CompilerParams(vmem_limit_bytes=56 * 2**20),
+        cost_estimate=pl.CostEstimate(
+            flops=20 * count * width * width, bytes_accessed=24 * count * width + 12 * width * width, transcendentals=0
+        ),
+        name="unproject",
+    )(x, before, sum1, gq, *gk, *gv, wq, wk, wv)
+
+
 def on_device(
     inputs,
     query_weight,
@@ -631,9 +707,16 @@
     qb, vb, ob, fg, fs, ub, sg, ss = [small_all[:, i] for i in range(8)]
     ib = small_all[:, 8:].reshape(hidden_width)
 
-    queries = (dot(flat_x, full_query) + qb).astype(BF16).reshape(micros, rows, width)
-    keys = [dot(t, full_key).astype(BF16).reshape(micros, -1, width) for t in key_x]
-    values = [(dot(t, full_value) + vb).astype(BF16).reshape(micros, -1, width) for t in key_x]
+    if seqs == 2:
+        queries, *kv = project(flat_x, key_x[1], full_query, full_key, full_value, qb, vb)
+        keys, values = kv[:2], kv[2:]
+    else:
+        queries = (dot(flat_x, full_query) + qb).astype(BF16)
+        keys = [dot(t, full_key).astype(BF16) for t in key_x]
+        values = [(dot(t, full_value) + vb).astype(BF16) for t in key_x]
+    queries = queries.reshape(micros, rows, width)
+    keys = [t.reshape(micros, -1, width) for t in keys]
+    values = [t.reshape(micros, -1, width) for t in values]
 
     mixed_parts, lse = attention(queries, keys, values, prefix[0])
     mixed = mixed_parts.reshape(micros * rows, width)
@@ -674,11 +757,21 @@
     grad_q = grad_q.reshape(micros * rows, width)
     grad_k = [t.reshape(-1, width) for t in grad_k]
     grad_v = [t.reshape(-1, width) for t in grad_v]
-    g_qbias = jnp.sum(grad_q.astype(F32), axis=0)
-    g_vbias = sum(jnp.sum(t.astype(F32), axis=0) for t in grad_v)
-    g_query = t_dot(flat_x, grad_q)
-    g_key = sum(t_dot(t, g) for t, g in zip(key_x, grad_k))
-    g_value = sum(t_dot(t, g) for t, g in zip(key_x, grad_v))
+    if seqs == 2:
+        grad_x, via_kv, g_query, g_key, g_value, sums = unproject(
+            flat_x, key_x[1], grad_sum1, grad_q, grad_k, grad_v, full_query, full_key, full_value
+        )
+        g_qbias, g_vbias = sums[0], sums[1]
+        sent = lax.ppermute(via_kv, "seq", [(1, 0)])
+    else:
+        g_qbias = jnp.sum(grad_q.astype(F32), axis=0)
+        g_vbias = sum(jnp.sum(t.astype(F32), axis=0) for t in grad_v)
+        g_query = t_dot(flat_x, grad_q)
+        g_key = sum(t_dot(t, g) for t, g in zip(key_x, grad_k))
+        g_value = sum(t_dot(t, g) for t, g in zip(key_x, grad_v))
+        via_kv = sum(dot_t(k, full_key) + dot_t(v, full_value) for k, v in zip(grad_k, grad_v))
+        grad_x = grad_sum1 + dot_t(grad_q, full_query)
+        sent = lax.psum_scatter(via_kv.reshape(micros, -1, width), "seq", scatter_dimension=1, tiled=True)
     g_small = jnp.concatenate(
         [
             jnp.stack([g_qbias, g_vbias, g_obias, g_fgain, g_fshift, g_ubias, g_sgain, g_sshift], axis=1),
@@ -690,14 +783,7 @@
     own_grads = scatter_all([g_outer, g_inner, g_output, g_query, g_key, g_value, g_small], 3)
     own_outer, own_inner, own_output, own_query, own_key, own_value, own_small = own_grads
 
-    via_kv = [dot_t(k, full_key) + dot_t(v, full_value) for k, v in zip(grad_k, grad_v)]
-    via_kv = [t.reshape(micros, -1, width) for t in via_kv]
-    grad_x = (grad_sum1 + dot_t(grad_q, full_query)).reshape(micros, rows, width)
-    if seqs == 2:
-        grad_x = grad_x + via_kv[0]
-        grad_x = grad_x + lax.ppermute(via_kv[1].astype(BF16), "seq", [(1, 0)]).astype(F32)
-    else:
-        grad_x = grad_x + lax.psum_scatter(via_kv[0], "seq", scatter_dimension=1, tiled=True)
+    grad_x = grad_x.reshape(micros, rows, width) + sent.reshape(micros, rows, width).astype(F32)
 
     vec = own_small[:, :small_count]
     v_of = [vec[:, i] for i in range(8)]

time: 425 us -> 412 us (0.969)
  matrix products: 108 us -> 60 us
  Pallas kernels: 261 us -> 297 us
    pallas_call x0 -> x2, Pallas kernels: none -> 29.2 us  [the longest x1 19.8 us: unproject(): pl.pallas_call(unproject_kernel, out_shape=[jax.ShapeDtypeStruct(x.shape,...]
    dot_general x8 -> x3, matrix products: 36.5 us -> 16.5 us  [dot(): return jnp.dot(a, b, preferred_element_type=F32)]
    dot_general x8 -> x3, matrix products: 38.4 us -> 19.4 us  [t_dot(): lax.dot_general(a, b, (((0,), (0,)), ((), ())), preferred_element_type=F32)]
    pallas_call x1, Pallas kernels: 89.3 us -> 101 us  [grid_scatter(): pl.pallas_call(functools.partial(scatter_kernel, count), out_shape=[jax.S...]
    convert_element_type x5 -> x0, local copies, waits for them, and re-layouts: 11.4 us -> none  [the longest x2 5.27 us: on_device(): (dot(t, full_value) + vb).astype(BF16).reshape(micros, -1, width)]
    dot_general x8 -> x3, matrix products: 33.4 us -> 24.1 us  [dot_t(): lax.dot_general(a, b, (((1,), (1,)), ((), ())), preferred_element_type=F32)]
    pallas_call x1, Pallas kernels: 98.9 us -> 93.1 us  [grid_gather(): pl.pallas_call(functools.partial(gather_kernel, count), out_shape=[jax.Sh...]
    another operation x8, local copies, waits for them, and re-layouts: 0.78 us -> 5.97 us  [on_device(): jnp.stack(vectors, axis=1)]
  transfers between devices with their start and end apart: 2 -> 2, of which waited for: 0 -> 0; matrix products, arithmetic and copies ran while one was open for 13% -> 8% of each run, Pallas kernels for 45% -> 48%
where the time goes in v1:
time: 412 us; the launch traced here: 408 us
  Pallas kernels  297 us (72%)
  matrix products  60 us (15%)
  local copies, waits for them, and re-layouts  30.5 us (7%)
  other arithmetic  16.2 us (4%)
    pallas_call x1, Pallas kernels, grid_scatter(): pl.pallas_call(functools.partial(scatter_kernel, count), out_shape=[jax.S...  101 us
    pallas_call x1, Pallas kernels, grid_gather(): pl.pallas_call(functools.partial(gather_kernel, count), out_shape=[jax.Sh...  93.1 us
    pallas_call x1, Pallas kernels, attention_back(): pl.pallas_call(functools.partial(backward_kernel, blocks), out_shape=[jax...  45 us
    pallas_call x1, Pallas kernels, attention(): pl.pallas_call(functools.partial(forward_kernel, blocks), out_shape=[jax....  27.9 us
    dot_general x3, matrix products, dot_t(): lax.dot_general(a, b, (((1,), (1,)), ((), ())), preferred_element_type=F32)  24.1 us
    pallas_call x1, Pallas kernels, unproject(): pl.pallas_call(unproject_kernel, out_shape=[jax.ShapeDtypeStruct(x.shape,...  19.8 us
    dot_general x3, matrix products, t_dot(): lax.dot_general(a, b, (((0,), (0,)), ((), ())), preferred_element_type=F32)  19.4 us
    dot_general x3, matrix products, dot(): return jnp.dot(a, b, preferred_element_type=F32)  16.5 us
  transfers between devices with their start and end apart: 2, of which 0 were waited for; matrix products, arithmetic and copies ran while one was open for 8% of the time, Pallas kernels for 48%

profile of v1, /device:TPU:12, one launch (start us, length us, event | category | flops | bytes accessed | tf_op | source)
XLA Modules:
  0.0 408.3 jit_solution(12633270495215977341)
XLA Ops:
  9.4 93.1 %grid_gather.1 = (bf16[32,24,768]{2,1,0:T(8,128)(2,1)}, bf16[32,24,768]{2,1,0:T(8,128)(2,1)}, bf16[32,24,768]{2,1,0:T(8,128)(2,1)}, bf16[32,24,128]{2,1,0:T(8,12...) custom-call(bf16[24,768]{1,0:T(8,128)(2,1)} %refs_0_.1, ...), custom_call_target="tpu_custom_call" | custom-call | tf_op jit(solution)/shard_map/grid_gather/pallas_call | solution.py:172
  102.6 1.8 copy.73
  108.6 2.3 reduce.4
  112.0 1.8 fusion.11
  115.1 9.4 %project.1 = (bf16[1024,768]{1,0:T(8,128)(2,1)S(1)}, bf16[1024,768]{1,0:T(8,128)(2,1)}, bf16[1024,768]{1,0:T(8,128)(2,1)}, bf16[1024,768]{1,0:T(8,128)(2,1)}, bf16[1024,768]{1,0:T(8,128)(2,1)}) custom-call(bf16[1024,768]{1,0:T(8,128)(2,1)} %bitcast.125, bf16[1024,768]{1,0:T(8,128)(2,1)} %bitcast.3.before_ref, bf16[768,768]{1,0:T(8,128)(2,1)S(1)} %bitcast.81, ...), custom_call_target="tpu_custom_call" | custom-call | flops 6039797760 | bytes 14548992 | tf_op jit(solution)/shard_map/project/pallas_call | solution.py:601
  124.5 2.0 copy-done.5
  126.5 27.9 %attention_forward.1 = (bf16[2,512,768]{2,1,0:T(8,128)(2,1)S(1)}, f32[2,6,8,512]{3,2,1,0:T(8,128)S(1)}) custom-call(s32[2]{0:T(128)S(1)} %bitcast.86, bf16[2,512,768]{2,1,0:T(8,128)(2,1)S(1)} %bitcast.88, bf16[2,512,768]{2,1,0:T(8,128)(2,1)S(1)} %bitcast.91, bf16[2,512,768]{2,1,0:T(8,128)(2,1)} %bitcast.130, bf16[2,512,768]{2,1,0:T(8,128)(2,1)} %bitcast.132, ...), custom_call_target="tpu_custom_call" | custom-call | flops 6442450944 | bytes 9437184 | tf_op jit(solution)/shard_map/attention_forward/pallas_call | solution.py:535
  154.4 1.6 fusion.22
  157.3 9.5 %multiply_convert_fusion = (bf16[1024,3072]{1,0:T(8,128)(2,1)S(1)}, f32[1024,3072]{1,0:T(8,128)}) fusion(f32[3072]{0:T(1024)S(1)} %add.109, bf16[768,3072]{1,0:T(8,128)(2,1)S(1)} %bitcast.118, f32[1024,768]{1,0:T(8,128)S(1)} %get-tuple-element.111, f32[768]{0:T(1024)S(1)} %get-tuple-element.90, f32[768]{0:T(1024)S(1)} %get-tuple-element.91, ...), kind=kOutput, calls=%fused_computation.7 | convolution fusion | flops 4854644736 | bytes 26765312 | tf_op jit(solution)/shard_map/dot_general | solution.py:370
  166.9 5.4 %fusion.23 = (f32[1024]{0:T(1024)S(1)}, f32[1024,768]{1,0:T(8,128)S(1)}) fusion(f32[768]{0:T(1024)S(1)} %get-tuple-element.89, bf16[1024,3072]{1,0:T(8,128)(2,1)S(1)} %get-tuple-element.112, bf16[3072,768]{1,0:T(8,128)(2,1)S(1)} %bitcast.122, f32[768]{0:T(1024)S(1)} %get-tuple-element.90, f32[768]{0:T(1024)S(1)} %get-tuple-element.91, ...), kind=kOutput, calls=%fused_computation.72 | convolution fusion | flops 4837342208 | bytes 17323008 | tf_op jit(solution)/shard_map/dot_general | solution.py:370
  173.7 2.7 fusion.12
  177.6 13.1 %fusion.24 = (bf16[3072]{0:T(1024)(128)(2,1)S(1)}, bf16[1024,3072]{1,0:T(8,128)(2,1)}) fusion(f32[1024,3072]{1,0:T(8,128)} %get-tuple-element.113, f32[3072]{0:T(1024)S(1)} %add.109, bf16[3072,768]{1,0:T(8,128)(2,1)S(1)} %bitcast.123, f32[1024,768]{1,0:T(8,128)S(1)} %get-tuple-element.102), kind=kOutput, calls=%fused_computation.73 | convolution fusion | flops 4876661760 | bytes 26757120 | tf_op jit(solution)/shard_map/dot_general | solution.py:374
  190.7 8.3 %multiply_reduce_fusion = (bf16[768]{0:T(1024)(128)(2,1)S(1)}, f32[1024]{0:T(1024)S(1)}, f32[1024]{0:T(1024)S(1)}, bf16[768]{0:T(1024)(128)(2,1)S(1)}, f32[1024,768]{1,0:T(8,128)S(1)}) fusion(f32[1024,768]{1,0:T(8,128)S(1)} %get-tuple-element.111, f32[1024]{0:T(1024)S(1)} %add_rsqrt_fusion.1, f32[1024]{0:T(1024)S(1)} %broadcast_multiply_fusion.4, ...), kind=kOutput, calls=%fused_computation.21 | convolution fusion | flops 4839698432 | bytes 20469760 | tf_op jit(solution)/shard_map/dot_general | solution.py:374
  199.0 1.6 convert_reduce_fusion
  200.6 2.7 convolution_convert_fusion.2
  203.3 2.5 convolution_convert_fusion.3
  205.8 7.0 %convolution_convert_fusion.1 = bf16[3072,768]{1,0:T(8,128)(2,1)} fusion(bf16[1024,3072]{1,0:T(8,128)(2,1)S(1)} %bitcast.140, f32[1024,768]{1,0:T(8,128)S(1)} %get-tuple-element.102), kind=kOutput, calls=%fused_computation.10 | convolution fusion | flops 4834983936 | bytes 14155776 | tf_op jit(solution)/shard_map/dot_general | solution.py:378
  212.9 45.0 %attention_backward.1 = (bf16[2,512,768]{2,1,0:T(8,128)(2,1)S(1)}, bf16[2,512,768]{2,1,0:T(8,128)(2,1)S(1)}, bf16[2,512,768]{2,1,0:T(8,128)(2,1)S(1)}, bf16[2,512,768]{2,1,0:T(8,128)(2,1)}, bf16[2,512,768]{2,1,0:T(8,128)(2,1)}) custom-call(s32[2]{0:T(128)S(1)} %bitcast.87, bf16[2,512,768]{2,1,0:T(8,128)(2,1)} %bitcast.89, bf16[2,512,768]{2,1,0:T(8,128)(2,1)} %copy-done.6, ...), custom_call_target="tpu_custom_call" | custom-call | flops 16106127360 | bytes 18874368 | tf_op jit(solution)/shard_map/attention_backward/pallas_call | solution.py:561
  261.4 19.8 %unproject.1 = (f32[1024,768]{1,0:T(8,128)}, bf16[1024,768]{1,0:T(8,128)(2,1)}, bf16[768,768]{1,0:T(8,128)(2,1)}, bf16[768,768]{1,0:T(8,128)(2,1)}, bf16[768,768]{1,0:T(8,128)(2,1)}, /*index=5*/f32[8,768]{1,0:T(8,128)}) custom-call(bf16[1024,768]{1,0:T(8,128)(2,1)} %bitcast.126, bf16[1024,768]{1,0:T(8,128)(2,1)} %bitcast.3.before_ref, ...), custom_call_target="tpu_custom_call" | custom-call | flops 12079595520 | bytes 25952256 | tf_op jit(solution)/shard_map/unproject/pallas_call | solution.py:647
  283.7 2.5 collective-permute-start.1
  286.1 9.9 %convolution_convert_fusion = bf16[768,3072]{1,0:T(8,128)(2,1)} fusion(bf16[1024,3072]{1,0:T(8,128)(2,1)} %get-tuple-element.118, f32[1024,768]{1,0:T(8,128)S(1)} %get-tuple-element.111, f32[768]{0:T(1024)S(1)} %copy-done.21, f32[768]{0:T(1024)S(1)} %get-tuple-element.91, f32[1024]{0:T(1024)S(1)} %add_rsqrt_fusion.1, f32[1024]{0:T(1024)S(1)} %broadcast_multiply_fusion.4), kind=kOutput, calls=%fused_computation.9 | convolution fusion | flops 4838129664 | bytes 14170112 | tf_op jit(solution)/shard_map/dot_general | solution.py:378
  296.0 101.4 %grid_scatter.1 = (f32[96,768]{1,0:T(8,128)}, f32[24,3072]{1,0:T(8,128)}, f32[24,768]{1,0:T(8,128)}, f32[24,768]{1,0:T(8,128)}, f32[24,768]{1,0:T(8,128)}, /*index=5*/f32[24,768]{1,0:T(8,128)}, f32[24,128]{1,0:T(8,128)}) custom-call(bf16[32,96,768]{2,1,0:T(8,128)(2,1)} %bitcast.97, bf16[32,24,3072]{2,1,0:T(8,128)(2,1)} %bitcast.98, ...), custom_call_target="tpu_custom_call" | custom-call | tf_op jit(solution)/shard_map/grid_scatter/pallas_call | solution.py:338
  398.8 1.8 slice_reduce_fusion
  400.7 3.4 convert_add_fusion
  (115 shorter events, 30.5 us)
Async XLA Ops:
  0.7 114.4 %collective-permute-start = (bf16[2,512,768]{2,1,0:T(8,128)(2,1)}, bf16[2,512,768]{2,1,0:T(8,128)(2,1)}, u32[]{:S(2)}, u32[]{:S(2)}) collective-permute-start(bf16[2,512,768]{2,1,0:T(8,128)(2,1)} %bitcast.124), channel_id=1, source_target_pairs={{0,16},{1,17},{2,18},{3,19},{4,20},{5,21},{6,22},{7,23},{8,24},{9,... | collective-permute-start | bytes 4718600 | tf_op jit(solution)/shard_map/ppermute | solution.py:693
  102.6 12.5 %copy-start = (bf16[32,24,768]{2,1,0:T(8,128)(2,1)S(1)}, bf16[32,24,768]{2,1,0:T(8,128)(2,1)}, u32[]{:S(2)}) copy-start(bf16[32,24,768]{2,1,0:T(8,128)(2,1)} %get-tuple-element.49) | copy-start | bytes 3538948
  102.6 12.5 %copy-start.1 = (bf16[32,24,768]{2,1,0:T(8,128)(2,1)S(1)}, bf16[32,24,768]{2,1,0:T(8,128)(2,1)}, u32[]{:S(2)}) copy-start(bf16[32,24,768]{2,1,0:T(8,128)(2,1)} %get-tuple-element.50) | copy-start | bytes 3538948
  102.6 12.5 %copy-start.2 = (bf16[32,24,768]{2,1,0:T(8,128)(2,1)S(1)}, bf16[32,24,768]{2,1,0:T(8,128)(2,1)}, u32[]{:S(2)}) copy-start(bf16[32,24,768]{2,1,0:T(8,128)(2,1)} %get-tuple-element.51) | copy-start | bytes 3538948
  112.0 54.8 %copy-start.20 = (f32[768]{0:T(1024)}, f32[768]{0:T(1024)S(1)}, u32[]{:S(2)}) copy-start(f32[768]{0:T(1024)S(1)} %get-tuple-element.90) | copy-start | bytes 9220
  115.1 9.4 %copy-start.3 = (s32[1,2]{1,0:T(1,128)S(1)}, s32[1,2]{1,0:T(1,128)}, u32[]{:S(2)}) copy-start(s32[1,2]{1,0:T(1,128)} %param.34) | copy-start | bytes 28
  124.5 29.9 %copy-start.4 = (bf16[1024,768]{1,0:T(8,128)(2,1)}, bf16[1024,768]{1,0:T(8,128)(2,1)S(1)}, u32[]{:S(2)}) copy-start(bf16[1024,768]{1,0:T(8,128)(2,1)S(1)} %get-tuple-element.53) | copy-start | bytes 4718596
  126.5 27.9 %copy-start.22 = (bf16[1,2,512,768]{3,2,1,0:T(8,128)(2,1)S(1)}, bf16[1,2,512,768]{3,2,1,0:T(8,128)(2,1)}, u32[]{:S(2)}) copy-start(bf16[1,2,512,768]{3,2,1,0:T(8,128)(2,1)} %param.18) | copy-start | bytes 4718596
  126.5 28.0 %copy-start.23 = (bf16[32,24,768]{2,1,0:T(8,128)(2,1)S(1)}, bf16[32,24,768]{2,1,0:T(8,128)(2,1)}, u32[]{:S(2)}) copy-start(bf16[32,24,768]{2,1,0:T(8,128)(2,1)} %get-tuple-element.59) | copy-start | bytes 3538948
  154.4 48.9 %copy-start.6 = (bf16[2,512,768]{2,1,0:T(8,128)(2,1)}, bf16[2,512,768]{2,1,0:T(8,128)(2,1)S(1)}, u32[]{:S(2)}) copy-start(bf16[2,512,768]{2,1,0:T(8,128)(2,1)S(1)} %get-tuple-element.58.o_ref) | copy-start | bytes 4718596
  156.0 10.8 %slice-start.2 = ((s8[4718592]{0:T(1024)(128)(4,1)}), s8[4194304]{0:T(1024)(128)(4,1)S(1)}, s32[]{:S(2)}) async-start(s8[4718592]{0:T(1024)(128)(4,1)} %bitcast.120), calls=%async_computation.2 | async-start | bytes 8388608
  157.3 9.6 %slice-start.3 = ((s8[4718592]{0:T(1024)(128)(4,1)}), s8[524288]{0:T(1024)(128)(4,1)S(1)}, s32[]{:S(2)}) async-start(s8[4718592]{0:T(1024)(128)(4,1)} %bitcast.120), calls=%async_computation.3 | async-start | bytes 1048576
  166.8 5.5 %copy-start.24 = (bf16[1024,3072]{1,0:T(8,128)(2,1)}, bf16[1024,3072]{1,0:T(8,128)(2,1)S(1)}, u32[]{:S(2)}) copy-start(bf16[1024,3072]{1,0:T(8,128)(2,1)S(1)} %get-tuple-element.112) | copy-start | bytes 18874372
  200.6 5.2 %slice-start.4 = ((s8[6291456]{0:T(1024)(128)(4,1)}), s8[4194304]{0:T(1024)(128)(4,1)S(1)}, s32[]{:S(2)}) async-start(s8[6291456]{0:T(1024)(128)(4,1)} %bitcast.139), calls=%async_computation.4 | async-start | bytes 8388608
  261.4 21.2 %copy-start.19 = (bf16[768,1]{0,1:T(2,128)(2,1)S(1)}, bf16[768,1]{0,1:T(2,128)(2,1)}, u32[]{:S(2)}) copy-start(bf16[768,1]{0,1:T(2,128)(2,1)} %stack.61) | copy-start | bytes 4612
  261.4 24.7 %copy-start.21 = (f32[768]{0:T(1024)S(1)}, f32[768]{0:T(1024)}, u32[]{:S(2)}) copy-start(f32[768]{0:T(1024)} %copy-done.20) | copy-start | bytes 9220
  283.7 117.0 %collective-permute-start.1 = (bf16[1024,768]{1,0:T(8,128)(2,1)}, bf16[1024,768]{1,0:T(8,128)(2,1)}, u32[]{:S(2)}, u32[]{:S(2)}) collective-permute-start(bf16[1024,768]{1,0:T(8,128)(2,1)} %get-tuple-element.69), channel_id=1, source_target_pairs={{16,0},{17,1},{18,2},{19,3},{20,4},{21,5},{22,6},{23,7},{24,8},{25... | collective-permute-start | bytes 4718600 | tf_op jit(solution)/shard_map/ppermute | solution.py:765
  296.0 104.6 %copy-start.11 = (f32[1024,768]{1,0:T(8,128)S(1)}, f32[1024,768]{1,0:T(8,128)}, u32[]{:S(2)}) copy-start(f32[1024,768]{1,0:T(8,128)} %get-tuple-element.68) | copy-start | bytes 9437188
  400.7 3.5 copy-start.18
  400.7 4.1 %copy-start.17 = (f32[24,768]{1,0:T(8,128)S(1)}, f32[24,768]{1,0:T(8,128)}, u32[]{:S(2)}) copy-start(f32[24,768]{1,0:T(8,128)} %get-tuple-element.141) | copy-start | bytes 221188
  400.7 4.8 %copy-start.16 = (f32[24,768]{1,0:T(8,128)S(1)}, f32[24,768]{1,0:T(8,128)}, u32[]{:S(2)}) copy-start(f32[24,768]{1,0:T(8,128)} %get-tuple-element.142) | copy-start | bytes 221188
  400.7 5.4 %copy-start.15 = (f32[24,768]{1,0:T(8,128)S(1)}, f32[24,768]{1,0:T(8,128)}, u32[]{:S(2)}) copy-start(f32[24,768]{1,0:T(8,128)} %get-tuple-element.145) | copy-start | bytes 221188
  400.7 6.0 %copy-start.14 = (f32[24,3072]{1,0:T(8,128)S(1)}, f32[24,3072]{1,0:T(8,128)}, u32[]{:S(2)}) copy-start(f32[24,3072]{1,0:T(8,128)} %get-tuple-element.149) | copy-start | bytes 884740
  400.7 6.7 %copy-start.13 = (f32[96,768]{1,0:T(8,128)S(1)}, f32[96,768]{1,0:T(8,128)}, u32[]{:S(2)}) copy-start(f32[96,768]{1,0:T(8,128)} %get-tuple-element.151) | copy-start | bytes 884740
  (9 other events, 17.8 us)

commit v2 on v1

--- a/solution.py
+++ b/solution.py
@@ -612,9 +612,31 @@
     )(x, before, wq, wk, wv, qb[None], vb[None])
 
 
+def return_kernel(gk_ref, gv_ref, wk_ref, wv_ref, via_ref):
+    via_ref[...] = (dot_t(gk_ref[...], wk_ref[...]) + dot_t(gv_ref[...], wv_ref[...])).astype(BF16)
+
+
+def returned(gk, gv, wk, wv):
+    count, width = gk.shape
+    rows = pl.BlockSpec((BLOCK, width), lambda i: (i, 0))
+    whole = pl.BlockSpec((width, width), lambda i: (0, 0))
+    return pl.pallas_call(
+        return_kernel,
+        out_shape=jax.ShapeDtypeStruct(gk.shape, BF16),
+        grid=(count // BLOCK,),
+        in_specs=[rows, rows, whole, whole],
+        out_specs=rows,
+        compiler_params=pltpu.CompilerParams(vmem_limit_bytes=48 * 2**20),
+        cost_estimate=pl.CostEstimate(
+            flops=4 * count * width * width, bytes_accessed=6 * count * width + 4 * width * width, transcendentals=0
+        ),
+        name="returned",
+    )(gk, gv, wk, wv)
+
+
 def unproject_kernel(
     x_ref, before_ref, sum1_ref, gq_ref, gk0_ref, gk1_ref, gv0_ref, gv1_ref, wq_ref, wk_ref, wv_ref,
-    gx_ref, via_ref, gwq_ref, gwk_ref, gwv_ref, sums_ref, acc_q, acc_k, acc_v,
+    gx_ref, gwq_ref, gwk_ref, gwv_ref, sums_ref, acc_q, acc_k, acc_v,
 ):
     step = pl.program_id(0)
 
@@ -625,7 +647,6 @@
 
     x, before = x_ref[...], before_ref[...]
     gq, gk0, gk1, gv0, gv1 = gq_ref[...], gk0_ref[...], gk1_ref[...], gv0_ref[...], gv1_ref[...]
-    via_ref[...] = (dot_t(gk1, wk_ref[...]) + dot_t(gv1, wv_ref[...])).astype(BF16)
     gx_ref[...] = sum1_ref[...] + dot_t(gq, wq_ref[...]) + dot_t(gk0, wk_ref[...]) + dot_t(gv0, wv_ref[...])
     acc_q[...] += t_dot(x, gq)
     acc_k[...] += t_dot(x, gk0) + t_dot(before, gk1)
@@ -646,16 +667,16 @@
     whole = pl.BlockSpec((width, width), lambda i: (0, 0))
     return pl.pallas_call(
         unproject_kernel,
-        out_shape=[jax.ShapeDtypeStruct(x.shape, F32), jax.ShapeDtypeStruct(x.shape, BF16)]
+        out_shape=[jax.ShapeDtypeStruct(x.shape, F32)]
         + [jax.ShapeDtypeStruct(wq.shape, BF16)] * 3
         + [jax.ShapeDtypeStruct((8, width), F32)],
         grid=(count // BLOCK,),
         in_specs=[rows] * 8 + [whole] * 3,
-        out_specs=[rows] * 2 + [whole] * 3 + [pl.BlockSpec((8, width), lambda i: (0, 0))],
+        out_specs=[rows] + [whole] * 3 + [pl.BlockSpec((8, width), lambda i: (0, 0))],
         scratch_shapes=[pltpu.VMEM(wq.shape, F32)] * 3,
         compiler_params=pltpu.CompilerParams(vmem_limit_bytes=56 * 2**20),
         cost_estimate=pl.CostEstimate(
-            flops=20 * count * width * width, bytes_accessed=24 * count * width + 12 * width * width, transcendentals=0
+            flops=16 * count * width * width, bytes_accessed=24 * count * width + 12 * width * width, transcendentals=0
         ),
         name="unproject",
     )(x, before, sum1, gq, *gk, *gv, wq, wk, wv)
@@ -758,11 +779,13 @@
     grad_k = [t.reshape(-1, width) for t in grad_k]
     grad_v = [t.reshape(-1, width) for t in grad_v]
     if seqs == 2:
-        grad_x, via_kv, g_query, g_key, g_value, sums = unproject(
+        via_kv = returned(grad_k[1], grad_v[1], full_key, full_value)
+        sent = lax.ppermute(via_kv, "seq", [(1, 0)])
+        grad_q, _ = lax.optimization_barrier((grad_q, via_kv))
+        grad_x, g_query, g_key, g_value, sums = unproject(
             flat_x, key_x[1], grad_sum1, grad_q, grad_k, grad_v, full_query, full_key, full_value
         )
         g_qbias, g_vbias = sums[0], sums[1]
-        sent = lax.ppermute(via_kv, "seq", [(1, 0)])
     else:
         g_qbias = jnp.sum(grad_q.astype(F32), axis=0)
         g_vbias = sum(jnp.sum(t.astype(F32), axis=0) for t in grad_v)

time: 412 us -> 387 us (0.939)
  Pallas kernels: 297 us -> 278 us
  local copies, waits for them, and re-layouts: 30.5 us -> 24.7 us
    pallas_call x1, Pallas kernels: 101 us -> 80.5 us  [grid_scatter(): pl.pallas_call(functools.partial(scatter_kernel, count), out_shape=[jax.S...]
    pallas_call x0 -> x1, Pallas kernels: none -> 4.81 us  [returned(): pl.pallas_call(return_kernel, out_shape=jax.ShapeDtypeStruct(gk.shape, BF...]
  transfers between devices with their start and end apart: 2 -> 2, of which waited for: 0 -> 0; matrix products, arithmetic and copies ran while one was open for 8% -> 7% of each run, Pallas kernels for 48% -> 50%
where the time goes in v2:
time: 387 us; the launch traced here: 382 us
  Pallas kernels  278 us (72%)
  matrix products  60.5 us (16%)
  local copies, waits for them, and re-layouts  24.7 us (6%)
  other arithmetic  14.9 us (4%)
    pallas_call x1, Pallas kernels, grid_gather(): pl.pallas_call(functools.partial(gather_kernel, count), out_shape=[jax.Sh...  93.1 us
    pallas_call x1, Pallas kernels, grid_scatter(): pl.pallas_call(functools.partial(scatter_kernel, count), out_shape=[jax.S...  80.5 us
    pallas_call x1, Pallas kernels, attention_back(): pl.pallas_call(functools.partial(backward_kernel, blocks), out_shape=[jax...  45 us
    pallas_call x1, Pallas kernels, attention(): pl.pallas_call(functools.partial(forward_kernel, blocks), out_shape=[jax....  27.9 us
    dot_general x3, matrix products, dot_t(): lax.dot_general(a, b, (((1,), (1,)), ((), ())), preferred_element_type=F32)  24 us
    dot_general x3, matrix products, t_dot(): lax.dot_general(a, b, (((0,), (0,)), ((), ())), preferred_element_type=F32)  20 us
    pallas_call x1, Pallas kernels, unproject(): pl.pallas_call(unproject_kernel, out_shape=[jax.ShapeDtypeStruct(x.shape,...  17.3 us
    dot_general x3, matrix products, dot(): return jnp.dot(a, b, preferred_element_type=F32)  16.5 us
  transfers between devices with their start and end apart: 2, of which 0 were waited for; matrix products, arithmetic and copies ran while one was open for 7% of the time, Pallas kernels for 50%

profile of v2, /device:TPU:12, one launch (start us, length us, event | category | flops | bytes accessed | tf_op | source)
XLA Modules:
  0.0 382.2 jit_solution(16564369681252866201)
XLA Ops:
  9.4 93.1 %grid_gather.1 = (bf16[32,24,768]{2,1,0:T(8,128)(2,1)}, bf16[32,24,768]{2,1,0:T(8,128)(2,1)}, bf16[32,24,768]{2,1,0:T(8,128)(2,1)}, bf16[32,24,128]{2,1,0:T(8,12...) custom-call(bf16[24,768]{1,0:T(8,128)(2,1)} %refs_0_.1, ...), custom_call_target="tpu_custom_call" | custom-call | tf_op jit(solution)/shard_map/grid_gather/pallas_call | solution.py:172
  104.2 1.7 reduce.4
  106.0 1.8 fusion.11
  109.1 9.4 %project.1 = (bf16[1024,768]{1,0:T(8,128)(2,1)S(1)}, bf16[1024,768]{1,0:T(8,128)(2,1)}, bf16[1024,768]{1,0:T(8,128)(2,1)}, bf16[1024,768]{1,0:T(8,128)(2,1)}, bf16[1024,768]{1,0:T(8,128)(2,1)}) custom-call(bf16[1024,768]{1,0:T(8,128)(2,1)} %bitcast.128, bf16[1024,768]{1,0:T(8,128)(2,1)} %bitcast.3.before_ref, bf16[768,768]{1,0:T(8,128)(2,1)S(1)} %bitcast.81, ...), custom_call_target="tpu_custom_call" | custom-call | flops 6039797760 | bytes 14548992 | tf_op jit(solution)/shard_map/project/pallas_call | solution.py:601
  118.5 2.0 copy-done.7
  120.5 27.9 %attention_forward.1 = (bf16[2,512,768]{2,1,0:T(8,128)(2,1)S(1)}, f32[2,6,8,512]{3,2,1,0:T(8,128)S(1)}) custom-call(s32[2]{0:T(128)S(1)} %bitcast.88, bf16[2,512,768]{2,1,0:T(8,128)(2,1)S(1)} %bitcast.90, bf16[2,512,768]{2,1,0:T(8,128)(2,1)S(1)} %bitcast.93, bf16[2,512,768]{2,1,0:T(8,128)(2,1)} %bitcast.133, bf16[2,512,768]{2,1,0:T(8,128)(2,1)} %bitcast.135, ...), custom_call_target="tpu_custom_call" | custom-call | flops 6442450944 | bytes 9437184 | tf_op jit(solution)/shard_map/attention_forward/pallas_call | solution.py:535
  148.4 1.6 fusion.22
  152.1 9.5 %multiply_convert_fusion = (bf16[1024,3072]{1,0:T(8,128)(2,1)S(1)}, f32[1024,3072]{1,0:T(8,128)}) fusion(f32[3072]{0:T(1024)S(1)} %add.109, bf16[768,3072]{1,0:T(8,128)(2,1)S(1)} %bitcast.121, f32[1024,768]{1,0:T(8,128)S(1)} %get-tuple-element.111, f32[768]{0:T(1024)S(1)} %get-tuple-element.90, f32[768]{0:T(1024)S(1)} %get-tuple-element.91, ...), kind=kOutput, calls=%fused_computation.7 | convolution fusion | flops 4854644736 | bytes 26765312 | tf_op jit(solution)/shard_map/dot_general | solution.py:370
  161.7 5.4 %fusion.23 = (f32[1024]{0:T(1024)S(1)}, f32[1024,768]{1,0:T(8,128)S(1)}) fusion(f32[768]{0:T(1024)S(1)} %get-tuple-element.89, bf16[1024,3072]{1,0:T(8,128)(2,1)S(1)} %get-tuple-element.112, bf16[3072,768]{1,0:T(8,128)(2,1)S(1)} %bitcast.125, f32[768]{0:T(1024)S(1)} %get-tuple-element.90, f32[768]{0:T(1024)S(1)} %get-tuple-element.91, ...), kind=kOutput, calls=%fused_computation.72 | convolution fusion | flops 4837342208 | bytes 17323008 | tf_op jit(solution)/shard_map/dot_general | solution.py:370
  168.5 2.7 fusion.12
  172.4 13.1 %fusion.24 = (bf16[3072]{0:T(1024)(128)(2,1)S(1)}, bf16[1024,3072]{1,0:T(8,128)(2,1)}) fusion(f32[1024,3072]{1,0:T(8,128)} %get-tuple-element.113, f32[3072]{0:T(1024)S(1)} %add.109, bf16[3072,768]{1,0:T(8,128)(2,1)S(1)} %bitcast.126, f32[1024,768]{1,0:T(8,128)S(1)} %get-tuple-element.102), kind=kOutput, calls=%fused_computation.73 | convolution fusion | flops 4876661760 | bytes 26757120 | tf_op jit(solution)/shard_map/dot_general | solution.py:374
  185.5 8.2 %multiply_reduce_fusion = (bf16[768]{0:T(1024)(128)(2,1)S(1)}, f32[1024]{0:T(1024)S(1)}, f32[1024]{0:T(1024)S(1)}, bf16[768]{0:T(1024)(128)(2,1)S(1)}, f32[1024,768]{1,0:T(8,128)S(1)}) fusion(f32[1024,768]{1,0:T(8,128)S(1)} %get-tuple-element.111, f32[1024]{0:T(1024)S(1)} %add_rsqrt_fusion.1, f32[1024]{0:T(1024)S(1)} %broadcast_multiply_fusion.4, ...), kind=kOutput, calls=%fused_computation.21 | convolution fusion | flops 4839698432 | bytes 20469760 | tf_op jit(solution)/shard_map/dot_general | solution.py:374
  193.8 1.6 convert_reduce_fusion
  195.4 2.7 convolution_convert_fusion.2
  198.1 2.6 convolution_convert_fusion.3
  200.7 7.0 %convolution_convert_fusion.1 = bf16[3072,768]{1,0:T(8,128)(2,1)} fusion(bf16[1024,3072]{1,0:T(8,128)(2,1)S(1)} %bitcast.144, f32[1024,768]{1,0:T(8,128)S(1)} %get-tuple-element.102), kind=kOutput, calls=%fused_computation.10 | convolution fusion | flops 4834983936 | bytes 14155776 | tf_op jit(solution)/shard_map/dot_general | solution.py:378
  207.6 45.0 %attention_backward.1 = (bf16[2,512,768]{2,1,0:T(8,128)(2,1)S(1)}, bf16[2,512,768]{2,1,0:T(8,128)(2,1)S(1)}, bf16[2,512,768]{2,1,0:T(8,128)(2,1)S(1)}, bf16[2,512,768]{2,1,0:T(8,128)(2,1)}, bf16[2,512,768]{2,1,0:T(8,128)(2,1)}) custom-call(s32[2]{0:T(128)S(1)} %bitcast.89, bf16[2,512,768]{2,1,0:T(8,128)(2,1)} %bitcast.91, bf16[2,512,768]{2,1,0:T(8,128)(2,1)} %copy-done.8, ...), custom_call_target="tpu_custom_call" | custom-call | flops 16106127360 | bytes 18874368 | tf_op jit(solution)/shard_map/attention_backward/pallas_call | solution.py:561
  253.8 4.8 %returned.1 = bf16[1024,768]{1,0:T(8,128)(2,1)S(1)} custom-call(bf16[1024,768]{1,0:T(8,128)(2,1)S(1)} %bitcast.98, bf16[1024,768]{1,0:T(8,128)(2,1)} %bitcast.140, bf16[768,768]{1,0:T(8,128)(2,1)S(1)} %bitcast.84, bf16[768,768]{1,0:T(8,128)(2,1)S(1)} %bitcast.87), custom_call_target="tpu_custom_call" | custom-call | flops 2415919104 | bytes 7077888 | tf_op jit(solution)/shard_map/returned/pallas_call | solution.py:623
  258.7 1.4 collective-permute-start.1
  260.1 17.3 %unproject.1 = (f32[1024,768]{1,0:T(8,128)}, bf16[768,768]{1,0:T(8,128)(2,1)}, bf16[768,768]{1,0:T(8,128)(2,1)}, bf16[768,768]{1,0:T(8,128)(2,1)}, f32[8,768]{1,0:T(8,128)}) custom-call(bf16[1024,768]{1,0:T(8,128)(2,1)} %bitcast.129, bf16[1024,768]{1,0:T(8,128)(2,1)} %bitcast.3.before_ref, f32[1024,768]{1,0:T(8,128)} %copy-done.14, ...), custom_call_target="tpu_custom_call" | custom-call | flops 9663676416 | bytes 25952256 | tf_op jit(solution)/shard_map/unproject/pallas_call | solution.py:668
  279.7 10.5 %convolution_convert_fusion = bf16[768,3072]{1,0:T(8,128)(2,1)} fusion(bf16[1024,3072]{1,0:T(8,128)(2,1)} %get-tuple-element.118, f32[1024,768]{1,0:T(8,128)} %copy-done.13, f32[768]{0:T(1024)S(1)} %get-tuple-element.90, f32[768]{0:T(1024)S(1)} %get-tuple-element.91, f32[1024]{0:T(1024)S(1)} %add_rsqrt_fusion.1, f32[1024]{0:T(1024)S(1)} %broadcast_multiply_fusion.4), kind=kOutput, calls=%fused_computation.9 | convolution fusion | flops 4838129664 | bytes 14170112 | tf_op jit(solution)/shard_map/dot_general | solution.py:378
  290.2 80.5 %grid_scatter.1 = (f32[96,768]{1,0:T(8,128)}, f32[24,3072]{1,0:T(8,128)}, f32[24,768]{1,0:T(8,128)}, f32[24,768]{1,0:T(8,128)}, f32[24,768]{1,0:T(8,128)}, /*index=5*/f32[24,768]{1,0:T(8,128)}, f32[24,128]{1,0:T(8,128)}) custom-call(bf16[32,96,768]{2,1,0:T(8,128)(2,1)} %bitcast.100, bf16[32,24,3072]{2,1,0:T(8,128)(2,1)} %bitcast.101, ...), custom_call_target="tpu_custom_call" | custom-call | tf_op jit(solution)/shard_map/grid_scatter/pallas_call | solution.py:338
  372.1 1.8 slice_reduce_fusion
  374.0 4.0 %convert_add_fusion = f32[1024,768]{1,0:T(8,128)} fusion(f32[1024,768]{1,0:T(8,128)} %get-tuple-element.69, bf16[1024,768]{1,0:T(8,128)(2,1)S(1)} %collective-permute-done.1), kind=kLoop, calls=%fused_computation.22 | loop fusion | flops 1572864 | bytes 7864320 | tf_op jit(solution)/shard_map/add | solution.py:809
  (116 shorter events, 25.2 us)
Async XLA Ops:
  0.7 107.1 %collective-permute-start = (bf16[2,512,768]{2,1,0:T(8,128)(2,1)}, bf16[2,512,768]{2,1,0:T(8,128)(2,1)}, u32[]{:S(2)}, u32[]{:S(2)}) collective-permute-start(bf16[2,512,768]{2,1,0:T(8,128)(2,1)} %bitcast.127), channel_id=1, source_target_pairs={{0,16},{1,17},{2,18},{3,19},{4,20},{5,21},{6,22},{7,23},{8,24},{9,... | collective-permute-start | bytes 4718600 | tf_op jit(solution)/shard_map/ppermute | solution.py:714
  102.6 5.2 %copy-start = (bf16[32,24,768]{2,1,0:T(8,128)(2,1)S(1)}, bf16[32,24,768]{2,1,0:T(8,128)(2,1)}, u32[]{:S(2)}) copy-start(bf16[32,24,768]{2,1,0:T(8,128)(2,1)} %get-tuple-element.49) | copy-start | bytes 3538948
  102.6 5.2 %copy-start.1 = (bf16[32,24,768]{2,1,0:T(8,128)(2,1)S(1)}, bf16[32,24,768]{2,1,0:T(8,128)(2,1)}, u32[]{:S(2)}) copy-start(bf16[32,24,768]{2,1,0:T(8,128)(2,1)} %get-tuple-element.50) | copy-start | bytes 3538948
  109.1 9.4 %copy-start.5 = (s32[1,2]{1,0:T(1,128)S(1)}, s32[1,2]{1,0:T(1,128)}, u32[]{:S(2)}) copy-start(s32[1,2]{1,0:T(1,128)} %param.34) | copy-start | bytes 28
  118.5 29.9 %copy-start.6 = (bf16[1024,768]{1,0:T(8,128)(2,1)}, bf16[1024,768]{1,0:T(8,128)(2,1)S(1)}, u32[]{:S(2)}) copy-start(bf16[1024,768]{1,0:T(8,128)(2,1)S(1)} %get-tuple-element.53) | copy-start | bytes 4718596
  120.5 27.9 %copy-start.21 = (bf16[1,2,512,768]{3,2,1,0:T(8,128)(2,1)S(1)}, bf16[1,2,512,768]{3,2,1,0:T(8,128)(2,1)}, u32[]{:S(2)}) copy-start(bf16[1,2,512,768]{3,2,1,0:T(8,128)(2,1)} %param.18) | copy-start | bytes 4718596
  120.5 27.9 %copy-start.22 = (bf16[32,24,768]{2,1,0:T(8,128)(2,1)S(1)}, bf16[32,24,768]{2,1,0:T(8,128)(2,1)}, u32[]{:S(2)}) copy-start(bf16[32,24,768]{2,1,0:T(8,128)(2,1)} %get-tuple-element.59) | copy-start | bytes 3538948
  148.4 49.7 %copy-start.8 = (bf16[2,512,768]{2,1,0:T(8,128)(2,1)}, bf16[2,512,768]{2,1,0:T(8,128)(2,1)S(1)}, u32[]{:S(2)}) copy-start(bf16[2,512,768]{2,1,0:T(8,128)(2,1)S(1)} %get-tuple-element.58.o_ref) | copy-start | bytes 4718596
  150.0 43.7 %copy-start.13 = (f32[1024,768]{1,0:T(8,128)}, f32[1024,768]{1,0:T(8,128)S(1)}, u32[]{:S(2)}) copy-start(f32[1024,768]{1,0:T(8,128)S(1)} %get-tuple-element.111) | copy-start | bytes 9437188
  150.0 11.6 %slice-start.2 = ((s8[4718592]{0:T(1024)(128)(4,1)}), s8[4194304]{0:T(1024)(128)(4,1)S(1)}, s32[]{:S(2)}) async-start(s8[4718592]{0:T(1024)(128)(4,1)} %bitcast.123), calls=%async_computation.2 | async-start | bytes 8388608
  152.1 9.5 %slice-start.3 = ((s8[4718592]{0:T(1024)(128)(4,1)}), s8[524288]{0:T(1024)(128)(4,1)S(1)}, s32[]{:S(2)}) async-start(s8[4718592]{0:T(1024)(128)(4,1)} %bitcast.123), calls=%async_computation.3 | async-start | bytes 1048576
  161.6 5.4 %copy-start.24 = (bf16[1024,3072]{1,0:T(8,128)(2,1)}, bf16[1024,3072]{1,0:T(8,128)(2,1)S(1)}, u32[]{:S(2)}) copy-start(bf16[1024,3072]{1,0:T(8,128)(2,1)S(1)} %get-tuple-element.112) | copy-start | bytes 18874372
  195.4 5.3 %slice-start.4 = ((s8[6291456]{0:T(1024)(128)(4,1)}), s8[4194304]{0:T(1024)(128)(4,1)S(1)}, s32[]{:S(2)}) async-start(s8[6291456]{0:T(1024)(128)(4,1)} %bitcast.143), calls=%async_computation.4 | async-start | bytes 8388608
  207.6 46.2 %copy-start.2 = (bf16[32,24,768]{2,1,0:T(8,128)(2,1)S(1)}, bf16[32,24,768]{2,1,0:T(8,128)(2,1)}, u32[]{:S(2)}) copy-start(bf16[32,24,768]{2,1,0:T(8,128)(2,1)} %get-tuple-element.50) | copy-start | bytes 3538948
  207.6 46.2 %copy-start.4 = (bf16[32,24,768]{2,1,0:T(8,128)(2,1)S(1)}, bf16[32,24,768]{2,1,0:T(8,128)(2,1)}, u32[]{:S(2)}) copy-start(bf16[32,24,768]{2,1,0:T(8,128)(2,1)} %get-tuple-element.51) | copy-start | bytes 3538948
  253.8 4.8 %copy-start.9 = (bf16[2,512,768]{2,1,0:T(8,128)(2,1)}, bf16[2,512,768]{2,1,0:T(8,128)(2,1)S(1)}, u32[]{:S(2)}) copy-start(bf16[2,512,768]{2,1,0:T(8,128)(2,1)S(1)} %get-tuple-element.63) | copy-start | bytes 4718596
  253.8 4.8 %copy-start.11 = (bf16[2,512,768]{2,1,0:T(8,128)(2,1)}, bf16[2,512,768]{2,1,0:T(8,128)(2,1)S(1)}, u32[]{:S(2)}) copy-start(bf16[2,512,768]{2,1,0:T(8,128)(2,1)S(1)} %get-tuple-element.64) | copy-start | bytes 4718596
  258.7 115.3 %collective-permute-start.1 = (bf16[1024,768]{1,0:T(8,128)(2,1)S(1)}, bf16[1024,768]{1,0:T(8,128)(2,1)S(1)}, u32[]{:S(2)}, u32[]{:S(2)}) collective-permute-start(bf16[1024,768]{1,0:T(8,128)(2,1)S(1)} %returned.1), channel_id=1, source_target_pairs={{16,0},{17,1},{18,2},{19,3},{20,4},{21,5},{22,6},{23,7},{24,8},{25... | collective-permute-start | bytes 4718600 | tf_op jit(solution)/shard_map/ppermute | solution.py:783
  373.9 4.1 %copy-start.20 = (f32[24,768]{1,0:T(8,128)S(1)}, f32[24,768]{1,0:T(8,128)}, u32[]{:S(2)}) copy-start(f32[24,768]{1,0:T(8,128)} %get-tuple-element.140) | copy-start | bytes 221188
  373.9 4.7 %copy-start.19 = (f32[24,768]{1,0:T(8,128)S(1)}, f32[24,768]{1,0:T(8,128)}, u32[]{:S(2)}) copy-start(f32[24,768]{1,0:T(8,128)} %get-tuple-element.141) | copy-start | bytes 221188
  373.9 5.3 %copy-start.18 = (f32[24,768]{1,0:T(8,128)S(1)}, f32[24,768]{1,0:T(8,128)}, u32[]{:S(2)}) copy-start(f32[24,768]{1,0:T(8,128)} %get-tuple-element.142) | copy-start | bytes 221188
  373.9 6.0 %copy-start.17 = (f32[24,768]{1,0:T(8,128)S(1)}, f32[24,768]{1,0:T(8,128)}, u32[]{:S(2)}) copy-start(f32[24,768]{1,0:T(8,128)} %get-tuple-element.145) | copy-start | bytes 221188
  374.0 6.6 %copy-start.16 = (f32[24,3072]{1,0:T(8,128)S(1)}, f32[24,3072]{1,0:T(8,128)}, u32[]{:S(2)}) copy-start(f32[24,3072]{1,0:T(8,128)} %get-tuple-element.149) | copy-start | bytes 884740
  374.0 7.3 %copy-start.15 = (f32[96,768]{1,0:T(8,128)S(1)}, f32[96,768]{1,0:T(8,128)}, u32[]{:S(2)}) copy-start(f32[96,768]{1,0:T(8,128)} %get-tuple-element.151) | copy-start | bytes 884740
  (9 other events, 19.7 us)

commit v3 on v2

--- a/solution.py
+++ b/solution.py
@@ -717,16 +717,18 @@
         key_x = [lax.all_gather(x, "seq", axis=1, tiled=True).reshape(-1, width)]
 
     vectors = (query_bias, value_bias, output_bias, first_gain, first_shift, outer_bias, second_gain, second_shift)
-    small = jnp.concatenate([jnp.stack(vectors, axis=1), inner_bias.reshape(own, per)], axis=1)
-    small_count = small.shape[1]
-    small = jnp.pad(small, ((0, 0), (0, 128 - small_count)))
+    lanes = lambda v: jnp.pad(v, ((0, 0),) * (v.ndim - 1) + ((0, 128 - v.shape[-1]),))
+    small = jnp.stack([lanes(v) for v in vectors + (inner_bias,)])
+    small = jnp.pad(small, ((0, 16 - small.shape[0]), (0, 0)))
     full = gather_all(
         [query_weight, key_weight, value_weight, small, output_weight, inner_weight, outer_weight], 1
     )
     full_query, full_key, full_value, small_all, full_output, full_inner, full_outer = full
-    small_all = small_all[:, :small_count].astype(F32)
-    qb, vb, ob, fg, fs, ub, sg, ss = [small_all[:, i] for i in range(8)]
-    ib = small_all[:, 8:].reshape(hidden_width)
+    small_all = small_all.reshape(-1, 16, 128)
+    shares = small_all.shape[0]
+    by_vector = small_all[:, :8, :own].transpose(1, 0, 2).reshape(8, width).astype(F32)
+    qb, vb, ob, fg, fs, ub, sg, ss = [by_vector[i] for i in range(8)]
+    ib = small_all[:, 8, : own * per].reshape(hidden_width).astype(F32)
 
     if seqs == 2:
         queries, *kv = project(flat_x, key_x[1], full_query, full_key, full_value, qb, vb)
@@ -795,21 +797,16 @@
         via_kv = sum(dot_t(k, full_key) + dot_t(v, full_value) for k, v in zip(grad_k, grad_v))
         grad_x = grad_sum1 + dot_t(grad_q, full_query)
         sent = lax.psum_scatter(via_kv.reshape(micros, -1, width), "seq", scatter_dimension=1, tiled=True)
-    g_small = jnp.concatenate(
-        [
-            jnp.stack([g_qbias, g_vbias, g_obias, g_fgain, g_fshift, g_ubias, g_sgain, g_sshift], axis=1),
-            g_ibias.reshape(width, per),
-        ],
-        axis=1,
-    )
-    g_small = jnp.pad(g_small, ((0, 0), (0, 128 - small_count)))
+    g_vectors = jnp.stack([g_qbias, g_vbias, g_obias, g_fgain, g_fshift, g_ubias, g_sgain, g_sshift])
+    g_vectors = lanes(g_vectors.reshape(8, shares, own).transpose(1, 0, 2).astype(BF16))
+    g_wide = lanes(g_ibias.reshape(shares, 1, own * per).astype(BF16))
+    g_small = jnp.pad(jnp.concatenate([g_vectors, g_wide], axis=1), ((0, 0), (0, 7), (0, 0))).reshape(-1, 128)
     own_grads = scatter_all([g_outer, g_inner, g_output, g_query, g_key, g_value, g_small], 3)
     own_outer, own_inner, own_output, own_query, own_key, own_value, own_small = own_grads
 
     grad_x = grad_x.reshape(micros, rows, width) + sent.reshape(micros, rows, width).astype(F32)
 
-    vec = own_small[:, :small_count]
-    v_of = [vec[:, i] for i in range(8)]
+    v_of = [own_small[i, :own] for i in range(8)]
     outputs = result.reshape(micros, rows, width)[None]
     return (
         outputs,
@@ -824,7 +821,7 @@
         v_of[3],
         v_of[4],
         own_inner,
-        vec[:, 8:].reshape(own * per),
+        own_small[8, : own * per],
         own_outer,
         v_of[5],
         v_of[6],

time: 387 us -> 387 us (level)
    unnamed x71 -> x63, local copies, waits for them, and re-layouts: 12.2 us -> 11 us
  transfers between devices with their start and end apart: 2 -> 2, of which waited for: 0 -> 0; matrix products, arithmetic and copies ran while one was open for 7% -> 7% of each run, Pallas kernels for 50% -> 51%
where the time goes in v3:
time: 387 us; the launch traced here: 383 us
  Pallas kernels  281 us (73%)
  matrix products  60.5 us (16%)
  local copies, waits for them, and re-layouts  21.2 us (5%)
  other arithmetic  15.5 us (4%)
    pallas_call x1, Pallas kernels, grid_gather(): pl.pallas_call(functools.partial(gather_kernel, count), out_shape=[jax.Sh...  96.3 us
    pallas_call x1, Pallas kernels, grid_scatter(): pl.pallas_call(functools.partial(scatter_kernel, count), out_shape=[jax.S...  80.3 us
    pallas_call x1, Pallas kernels, attention_back(): pl.pallas_call(functools.partial(backward_kernel, blocks), out_shape=[jax...  45 us
    pallas_call x1, Pallas kernels, attention(): pl.pallas_call(functools.partial(forward_kernel, blocks), out_shape=[jax....  27.9 us
    dot_general x3, matrix products, dot_t(): lax.dot_general(a, b, (((1,), (1,)), ((), ())), preferred_element_type=F32)  24.1 us
    dot_general x3, matrix products, t_dot(): lax.dot_general(a, b, (((0,), (0,)), ((), ())), preferred_element_type=F32)  20 us
    pallas_call x1, Pallas kernels, unproject(): pl.pallas_call(unproject_kernel, out_shape=[jax.ShapeDtypeStruct(x.shape,...  17.5 us
    dot_general x3, matrix products, dot(): return jnp.dot(a, b, preferred_element_type=F32)  16.4 us
  transfers between devices with their start and end apart: 2, of which 0 were waited for; matrix products, arithmetic and copies ran while one was open for 7% of the time, Pallas kernels for 51%

profile of v3, /device:TPU:12, one launch (start us, length us, event | category | flops | bytes accessed | tf_op | source)
XLA Modules:
  0.0 382.7 jit_solution(5665932193023853503)
XLA Ops:
  0.7 1.3 collective-permute-start
  6.0 96.3 %grid_gather.1 = (bf16[32,24,768]{2,1,0:T(8,128)(2,1)}, bf16[32,24,768]{2,1,0:T(8,128)(2,1)}, bf16[32,24,768]{2,1,0:T(8,128)(2,1)}, bf16[32,16,128]{2,1,0:T(8,12...) custom-call(bf16[24,768]{1,0:T(8,128)(2,1)} %refs_0_.1, ...), custom_call_target="tpu_custom_call" | custom-call | tf_op jit(solution)/shard_map/grid_gather/pallas_call | solution.py:172
  105.4 1.7 reduce.5
  107.1 1.8 fusion.11
  110.3 9.4 %project.1 = (bf16[1024,768]{1,0:T(8,128)(2,1)S(1)}, bf16[1024,768]{1,0:T(8,128)(2,1)}, bf16[1024,768]{1,0:T(8,128)(2,1)}, bf16[1024,768]{1,0:T(8,128)(2,1)}, bf16[1024,768]{1,0:T(8,128)(2,1)}) custom-call(bf16[1024,768]{1,0:T(8,128)(2,1)} %bitcast.139, bf16[1024,768]{1,0:T(8,128)(2,1)} %bitcast.3.before_ref, bf16[768,768]{1,0:T(8,128)(2,1)S(1)} %bitcast.101, ...), custom_call_target="tpu_custom_call" | custom-call | flops 6039797760 | bytes 14548992 | tf_op jit(solution)/shard_map/project/pallas_call | solution.py:601
  119.7 2.0 copy-done.7
  121.7 27.9 %attention_forward.1 = (bf16[2,512,768]{2,1,0:T(8,128)(2,1)S(1)}, f32[2,6,8,512]{3,2,1,0:T(8,128)S(1)}) custom-call(s32[2]{0:T(128)S(1)} %bitcast.108, bf16[2,512,768]{2,1,0:T(8,128)(2,1)S(1)} %bitcast.110, bf16[2,512,768]{2,1,0:T(8,128)(2,1)S(1)} %bitcast.113, bf16[2,512,768]{2,1,0:T(8,128)(2,1)} %bitcast.144, bf16[2,512,768]{2,1,0:T(8,128)(2,1)} %bitcast.146, ...), custom_call_target="tpu_custom_call" | custom-call | flops 6442450944 | bytes 9437184 | tf_op jit(solution)/shard_map/attention_forward/pallas_call | solution.py:535
  149.7 1.6 fusion.25
  153.3 9.4 %multiply_convert_fusion = (bf16[1024,3072]{1,0:T(8,128)(2,1)S(1)}, f32[1024,3072]{1,0:T(8,128)}) fusion(f32[3072]{0:T(1024)S(1)} %reshape.269, bf16[768,3072]{1,0:T(8,128)(2,1)S(1)} %bitcast.132, f32[1024,768]{1,0:T(8,128)S(1)} %get-tuple-element.109, f32[768]{0:T(1024)S(1)} %add.126, f32[768]{0:T(1024)S(1)} %mul.138, f32[1024]{0:T(1024)S(1)} %add_rsqrt_fusion.1, ...), kind=kOutput, calls=%fused_computation.7 | convolution fusion | flops 4854644736 | bytes 26765312 | tf_op jit(solution)/shard_map/dot_general | solution.py:370
  162.8 5.4 %fusion.26 = (f32[1024]{0:T(1024)S(1)}, f32[1024,768]{1,0:T(8,128)S(1)}) fusion(f32[768]{0:T(1024)S(1)} %add.134, bf16[1024,3072]{1,0:T(8,128)(2,1)S(1)} %get-tuple-element.110, bf16[3072,768]{1,0:T(8,128)(2,1)S(1)} %bitcast.136, f32[768]{0:T(1024)S(1)} %add.126, f32[768]{0:T(1024)S(1)} %mul.138, f32[1024]{0:T(1024)S(1)} %add_rsqrt_fusion.1, ...), kind=kOutput, calls=%fused_computation.88 | convolution fusion | flops 4837342208 | bytes 17323008 | tf_op jit(solution)/shard_map/dot_general | solution.py:370
  169.6 2.7 fusion.12
  173.5 7.1 %convolution_convert_fusion.1 = bf16[3072,768]{1,0:T(8,128)(2,1)} fusion(bf16[1024,3072]{1,0:T(8,128)(2,1)S(1)} %get-tuple-element.110, f32[1024,768]{1,0:T(8,128)S(1)} %get-tuple-element.96), kind=kOutput, calls=%fused_computation.10 | convolution fusion | flops 4834983936 | bytes 14155776 | tf_op jit(solution)/shard_map/dot_general | solution.py:378
  180.6 13.0 %fusion.27 = (bf16[3072]{0:T(1024)(128)(2,1)S(1)}, bf16[1024,3072]{1,0:T(8,128)(2,1)}) fusion(f32[1024,3072]{1,0:T(8,128)} %get-tuple-element.111, f32[3072]{0:T(1024)S(1)} %reshape.269, bf16[3072,768]{1,0:T(8,128)(2,1)S(1)} %bitcast.137, f32[1024,768]{1,0:T(8,128)S(1)} %get-tuple-element.96), kind=kOutput, calls=%fused_computation.89 | convolution fusion | flops 4876661760 | bytes 26757120 | tf_op jit(solution)/shard_map/dot_general | solution.py:374
  193.7 8.5 %multiply_reduce_fusion = (bf16[768]{0:T(1024)(128)(2,1)S(1)}, f32[1024]{0:T(1024)S(1)}, f32[1024]{0:T(1024)S(1)}, bf16[768]{0:T(1024)(128)(2,1)S(1)}, f32[1024,768]{1,0:T(8,128)S(1)}) fusion(f32[1024,768]{1,0:T(8,128)S(1)} %get-tuple-element.109, f32[1024]{0:T(1024)S(1)} %add_rsqrt_fusion.1, f32[1024]{0:T(1024)S(1)} %broadcast_multiply_fusion.4, ...), kind=kOutput, calls=%fused_computation.21 | convolution fusion | flops 4839698432 | bytes 20469760 | tf_op jit(solution)/shard_map/dot_general | solution.py:374
  203.5 2.6 convolution_convert_fusion.2
  206.1 2.5 convolution_convert_fusion.3
  208.6 45.0 %attention_backward.1 = (bf16[2,512,768]{2,1,0:T(8,128)(2,1)S(1)}, bf16[2,512,768]{2,1,0:T(8,128)(2,1)S(1)}, bf16[2,512,768]{2,1,0:T(8,128)(2,1)S(1)}, bf16[2,512,768]{2,1,0:T(8,128)(2,1)}, bf16[2,512,768]{2,1,0:T(8,128)(2,1)}) custom-call(s32[2]{0:T(128)S(1)} %bitcast.109, bf16[2,512,768]{2,1,0:T(8,128)(2,1)} %bitcast.111, bf16[2,512,768]{2,1,0:T(8,128)(2,1)} %copy-done.8, ...), custom_call_target="tpu_custom_call" | custom-call | flops 16106127360 | bytes 18874368 | tf_op jit(solution)/shard_map/attention_backward/pallas_call | solution.py:561
  254.8 4.8 %returned.1 = bf16[1024,768]{1,0:T(8,128)(2,1)S(1)} custom-call(bf16[1024,768]{1,0:T(8,128)(2,1)S(1)} %bitcast.118, bf16[1024,768]{1,0:T(8,128)(2,1)} %bitcast.151, bf16[768,768]{1,0:T(8,128)(2,1)S(1)} %bitcast.104, bf16[768,768]{1,0:T(8,128)(2,1)S(1)} %bitcast.107), custom_call_target="tpu_custom_call" | custom-call | flops 2415919104 | bytes 7077888 | tf_op jit(solution)/shard_map/returned/pallas_call | solution.py:623
  259.6 1.4 collective-permute-start.1
  261.0 17.5 %unproject.1 = (f32[1024,768]{1,0:T(8,128)}, bf16[768,768]{1,0:T(8,128)(2,1)}, bf16[768,768]{1,0:T(8,128)(2,1)}, bf16[768,768]{1,0:T(8,128)(2,1)}, f32[8,768]{1,0:T(8,128)}) custom-call(bf16[1024,768]{1,0:T(8,128)(2,1)} %bitcast.140, bf16[1024,768]{1,0:T(8,128)(2,1)} %bitcast.3.before_ref, f32[1024,768]{1,0:T(8,128)} %copy-done.14, ...), custom_call_target="tpu_custom_call" | custom-call | flops 9663676416 | bytes 25952256 | tf_op jit(solution)/shard_map/unproject/pallas_call | solution.py:668
  280.9 10.4 %convolution_convert_fusion = bf16[768,3072]{1,0:T(8,128)(2,1)} fusion(bf16[1024,3072]{1,0:T(8,128)(2,1)} %get-tuple-element.116, f32[1024,768]{1,0:T(8,128)} %copy-done.13, f32[768]{0:T(1024)S(1)} %add.126, f32[768]{0:T(1024)S(1)} %mul.138, f32[1024]{0:T(1024)S(1)} %add_rsqrt_fusion.1, f32[1024]{0:T(1024)S(1)} %broadcast_multiply_fusion.4), kind=kOutput, calls=%fused_computation.9 | convolution fusion | flops 4838129664 | bytes 14170112 | tf_op jit(solution)/shard_map/dot_general | solution.py:378
  291.3 80.3 %grid_scatter.1 = (f32[96,768]{1,0:T(8,128)}, f32[24,3072]{1,0:T(8,128)}, f32[24,768]{1,0:T(8,128)}, f32[24,768]{1,0:T(8,128)}, f32[24,768]{1,0:T(8,128)}, /*index=5*/f32[24,768]{1,0:T(8,128)}, f32[16,128]{1,0:T(8,128)}) custom-call(bf16[32,96,768]{2,1,0:T(8,128)(2,1)} %bitcast.120, bf16[32,24,3072]{2,1,0:T(8,128)(2,1)} %bitcast.121, ...), custom_call_target="tpu_custom_call" | custom-call | tf_op jit(solution)/shard_map/grid_scatter/pallas_call | solution.py:338
  372.8 1.5 slice_bitcast_fusion
  374.4 3.9 %convert_add_fusion = f32[1024,768]{1,0:T(8,128)} fusion(f32[1024,768]{1,0:T(8,128)} %get-tuple-element.69, bf16[1024,768]{1,0:T(8,128)(2,1)S(1)} %collective-permute-done.1), kind=kLoop, calls=%fused_computation.22 | loop fusion | flops 1572864 | bytes 7864320 | tf_op jit(solution)/shard_map/add | solution.py:807
  (111 shorter events, 23.0 us)
Async XLA Ops:
  0.7 108.3 %collective-permute-start = (bf16[2,512,768]{2,1,0:T(8,128)(2,1)}, bf16[2,512,768]{2,1,0:T(8,128)(2,1)}, u32[]{:S(2)}, u32[]{:S(2)}) collective-permute-start(bf16[2,512,768]{2,1,0:T(8,128)(2,1)} %bitcast.138), channel_id=1, source_target_pairs={{0,16},{1,17},{2,18},{3,19},{4,20},{5,21},{6,22},{7,23},{8,24},{9,... | collective-permute-start | bytes 4718600 | tf_op jit(solution)/shard_map/ppermute | solution.py:714
  102.3 6.7 %copy-start = (bf16[32,24,768]{2,1,0:T(8,128)(2,1)S(1)}, bf16[32,24,768]{2,1,0:T(8,128)(2,1)}, u32[]{:S(2)}) copy-start(bf16[32,24,768]{2,1,0:T(8,128)(2,1)} %get-tuple-element.49) | copy-start | bytes 3538948
  102.3 6.7 %copy-start.1 = (bf16[32,24,768]{2,1,0:T(8,128)(2,1)S(1)}, bf16[32,24,768]{2,1,0:T(8,128)(2,1)}, u32[]{:S(2)}) copy-start(bf16[32,24,768]{2,1,0:T(8,128)(2,1)} %get-tuple-element.50) | copy-start | bytes 3538948
  110.3 9.4 %copy-start.5 = (s32[1,2]{1,0:T(1,128)S(1)}, s32[1,2]{1,0:T(1,128)}, u32[]{:S(2)}) copy-start(s32[1,2]{1,0:T(1,128)} %param.34) | copy-start | bytes 28
  119.7 29.9 %copy-start.6 = (bf16[1024,768]{1,0:T(8,128)(2,1)}, bf16[1024,768]{1,0:T(8,128)(2,1)S(1)}, u32[]{:S(2)}) copy-start(bf16[1024,768]{1,0:T(8,128)(2,1)S(1)} %get-tuple-element.53) | copy-start | bytes 4718596
  121.7 28.0 %copy-start.21 = (bf16[1,2,512,768]{3,2,1,0:T(8,128)(2,1)S(1)}, bf16[1,2,512,768]{3,2,1,0:T(8,128)(2,1)}, u32[]{:S(2)}) copy-start(bf16[1,2,512,768]{3,2,1,0:T(8,128)(2,1)} %param.18) | copy-start | bytes 4718596
  121.7 28.0 %copy-start.22 = (bf16[32,24,768]{2,1,0:T(8,128)(2,1)S(1)}, bf16[32,24,768]{2,1,0:T(8,128)(2,1)}, u32[]{:S(2)}) copy-start(bf16[32,24,768]{2,1,0:T(8,128)(2,1)} %get-tuple-element.59) | copy-start | bytes 3538948
  149.6 56.5 %copy-start.8 = (bf16[2,512,768]{2,1,0:T(8,128)(2,1)}, bf16[2,512,768]{2,1,0:T(8,128)(2,1)S(1)}, u32[]{:S(2)}) copy-start(bf16[2,512,768]{2,1,0:T(8,128)(2,1)S(1)} %get-tuple-element.58.o_ref) | copy-start | bytes 4718596
  149.6 3.2 slice-start
  149.7 3.7 slice-start.1
  151.3 51.0 %copy-start.13 = (f32[1024,768]{1,0:T(8,128)}, f32[1024,768]{1,0:T(8,128)S(1)}, u32[]{:S(2)}) copy-start(f32[1024,768]{1,0:T(8,128)S(1)} %get-tuple-element.109) | copy-start | bytes 9437188
  151.3 11.4 %slice-start.2 = ((s8[4718592]{0:T(1024)(128)(4,1)}), s8[4194304]{0:T(1024)(128)(4,1)S(1)}, s32[]{:S(2)}) async-start(s8[4718592]{0:T(1024)(128)(4,1)} %bitcast.134), calls=%async_computation.2 | async-start | bytes 8388608
  153.3 9.4 %slice-start.3 = ((s8[4718592]{0:T(1024)(128)(4,1)}), s8[524288]{0:T(1024)(128)(4,1)S(1)}, s32[]{:S(2)}) async-start(s8[4718592]{0:T(1024)(128)(4,1)} %bitcast.134), calls=%async_computation.3 | async-start | bytes 1048576
  208.6 46.2 %copy-start.2 = (bf16[32,24,768]{2,1,0:T(8,128)(2,1)S(1)}, bf16[32,24,768]{2,1,0:T(8,128)(2,1)}, u32[]{:S(2)}) copy-start(bf16[32,24,768]{2,1,0:T(8,128)(2,1)} %get-tuple-element.50) | copy-start | bytes 3538948
  208.6 46.2 %copy-start.4 = (bf16[32,24,768]{2,1,0:T(8,128)(2,1)S(1)}, bf16[32,24,768]{2,1,0:T(8,128)(2,1)}, u32[]{:S(2)}) copy-start(bf16[32,24,768]{2,1,0:T(8,128)(2,1)} %get-tuple-element.51) | copy-start | bytes 3538948
  254.8 4.8 %copy-start.9 = (bf16[2,512,768]{2,1,0:T(8,128)(2,1)}, bf16[2,512,768]{2,1,0:T(8,128)(2,1)S(1)}, u32[]{:S(2)}) copy-start(bf16[2,512,768]{2,1,0:T(8,128)(2,1)S(1)} %get-tuple-element.63) | copy-start | bytes 4718596
  254.8 4.8 %copy-start.11 = (bf16[2,512,768]{2,1,0:T(8,128)(2,1)}, bf16[2,512,768]{2,1,0:T(8,128)(2,1)S(1)}, u32[]{:S(2)}) copy-start(bf16[2,512,768]{2,1,0:T(8,128)(2,1)S(1)} %get-tuple-element.64) | copy-start | bytes 4718596
  259.6 114.7 %collective-permute-start.1 = (bf16[1024,768]{1,0:T(8,128)(2,1)S(1)}, bf16[1024,768]{1,0:T(8,128)(2,1)S(1)}, u32[]{:S(2)}, u32[]{:S(2)}) collective-permute-start(bf16[1024,768]{1,0:T(8,128)(2,1)S(1)} %returned.1), channel_id=1, source_target_pairs={{16,0},{17,1},{18,2},{19,3},{20,4},{21,5},{22,6},{23,7},{24,8},{25... | collective-permute-start | bytes 4718600 | tf_op jit(solution)/shard_map/ppermute | solution.py:785
  374.3 4.0 %copy-start.20 = (f32[24,768]{1,0:T(8,128)S(1)}, f32[24,768]{1,0:T(8,128)}, u32[]{:S(2)}) copy-start(f32[24,768]{1,0:T(8,128)} %get-tuple-element.144) | copy-start | bytes 221188
  374.3 4.6 %copy-start.19 = (f32[24,768]{1,0:T(8,128)S(1)}, f32[24,768]{1,0:T(8,128)}, u32[]{:S(2)}) copy-start(f32[24,768]{1,0:T(8,128)} %get-tuple-element.145) | copy-start | bytes 221188
  374.3 5.2 %copy-start.18 = (f32[24,768]{1,0:T(8,128)S(1)}, f32[24,768]{1,0:T(8,128)}, u32[]{:S(2)}) copy-start(f32[24,768]{1,0:T(8,128)} %get-tuple-element.146) | copy-start | bytes 221188
  374.4 5.9 %copy-start.17 = (f32[24,768]{1,0:T(8,128)S(1)}, f32[24,768]{1,0:T(8,128)}, u32[]{:S(2)}) copy-start(f32[24,768]{1,0:T(8,128)} %get-tuple-element.149) | copy-start | bytes 221188
  374.4 6.5 %copy-start.16 = (f32[24,3072]{1,0:T(8,128)S(1)}, f32[24,3072]{1,0:T(8,128)}, u32[]{:S(2)}) copy-start(f32[24,3072]{1,0:T(8,128)} %get-tuple-element.153) | copy-start | bytes 884740
  374.4 7.2 %copy-start.15 = (f32[96,768]{1,0:T(8,128)S(1)}, f32[96,768]{1,0:T(8,128)}, u32[]{:S(2)}) copy-start(f32[96,768]{1,0:T(8,128)} %get-tuple-element.155) | copy-start | bytes 884740
  (6 other events, 9.9 us)
